TPU v7x, 64 devices: a 2x2x8 block of a 4x4x8 slice. The times are simulated.
64 devices in a mesh: tp: 4 (over x, y), cp: 16 (over z, core).
Axes of the slice: x: 2, y: 2, z: 8, core: 2. Of those that a mesh axis runs over, the one named last changes fastest.
The devices are a block of a 4x4x8 slice.
Arguments:
- query: bfloat16 [16, 512, 32, 128], P(None, 'cp', 'tp'), parts along dimension 2
- out_act: bfloat16 [16, 512, 32, 128], P(None, 'cp', 'tp'), parts along dimension 2
- out_grad: bfloat16 [16, 512, 32, 128], P(None, 'cp', 'tp'), parts along dimension 2
- row_lse: float32 [16, 512, 32], P(None, 'cp', 'tp'), parts along dimension 2
- key_act: bfloat16 [10240, 8, 128], P('cp', 'tp'), parts along dimension 1
- value_act: bfloat16 [10240, 8, 128], P('cp', 'tp'), parts along dimension 1
- doc_ids: int32 [10240], replicated
Outputs:
- output 1: bfloat16 [16, 512, 32, 128], P(None, 'cp', 'tp'), parts along dimension 2
- output 2: float32 [10240, 8, 128], P('cp', 'tp'), parts along dimension 1
- output 3: float32 [10240, 8, 128], P('cp', 'tp'), parts along dimension 1
There are 4 independent parts. A program takes and returns all parts, laid end to end along the dimension named above; an argument that names none is the same for every part.
All inputs are finite; a program needn't handle non-finite values.
Results may differ from a plain program's by a relative error of at most 0.00747609.
Values are sent between devices in bfloat16 or wider.
A program may use at most 768 MiB of HBM per device.

v0:
```python
import jax
import jax.numpy as jnp
from jax import lax
from jax.sharding import PartitionSpec as P


def solution(mesh):
    cp_size = mesh.shape['cp']
    q_spec = P(None, 'cp', 'tp', None)
    lse_spec = P(None, 'cp', 'tp')
    kv_spec = P('cp', 'tp', None)

    def local_backward(query, out_act, out_grad, row_lse, key_act, value_act, doc_ids):
        n_sub, local_len, n_heads, head_dim = query.shape
        keys_local, n_kv = key_act.shape[0], key_act.shape[1]
        group_size = n_heads // n_kv
        sub_len = local_len * cp_size
        sub_start = keys_local * cp_size - n_sub * sub_len
        score_scale = head_dim ** -0.5
        key_first = lax.axis_index('cp') * keys_local
        key_pos = key_first + jnp.arange(keys_local)
        key_doc = lax.dynamic_slice(doc_ids, (key_first,), (keys_local,))
        grp_shape = (n_sub, local_len, n_kv, group_size, head_dim)
        q_grp = query.reshape(grp_shape)
        do_grp = out_grad.reshape(grp_shape)
        row_delta = jnp.einsum('sqhgd,sqhgd->sqhg', do_grp, out_act.reshape(grp_shape), preferred_element_type=jnp.float32)
        row_stats = jnp.stack([row_lse.reshape(n_sub, local_len, n_kv, group_size), row_delta], axis=-1)
        firsts = sub_start + jnp.arange(n_sub) * sub_len

        def sub_step(carry_in, xs_sub):
            dk_acc, dv_acc = carry_in
            q_loc, do_loc, stats_loc, first_pos = xs_sub
            q_all = lax.all_gather(q_loc, 'cp', axis=0, tiled=True)
            do_all = lax.all_gather(do_loc, 'cp', axis=0, tiled=True)
            stats_all = lax.all_gather(stats_loc, 'cp', axis=0, tiled=True)
            q_pos = first_pos + jnp.arange(sub_len)
            q_doc = lax.dynamic_slice(doc_ids, (first_pos,), (sub_len,))
            allowed = (key_pos[None, :] <= q_pos[:, None]) & (key_doc[None, :] == q_doc[:, None])
            scores = jnp.einsum('qhgd,khd->qhgk', q_all, key_act, preferred_element_type=jnp.float32) * score_scale
            p_full = jnp.where(allowed[:, None, None, :], jnp.exp(scores - stats_all[..., 0:1]), 0.0)
            dv_acc = dv_acc + jnp.einsum('qhgk,qhgd->khd', p_full.astype(jnp.bfloat16), do_all, preferred_element_type=jnp.float32)
            d_prob = jnp.einsum('qhgd,khd->qhgk', do_all, value_act, preferred_element_type=jnp.float32)
            d_score = (p_full * (d_prob - stats_all[..., 1:2])).astype(jnp.bfloat16)
            dk_acc = dk_acc + jnp.einsum('qhgk,qhgd->khd', d_score, q_all, preferred_element_type=jnp.float32) * score_scale
            dq_part = jnp.einsum('qhgk,khd->qhgd', d_score, key_act, preferred_element_type=jnp.float32) * score_scale
            dq_sum = lax.psum_scatter(dq_part, 'cp', scatter_dimension=0, tiled=True)
            return (dk_acc, dv_acc), dq_sum.astype(jnp.bfloat16).reshape(local_len, n_heads, head_dim)

        zero_acc = jnp.zeros((keys_local, n_kv, head_dim), jnp.float32)
        (d_key, d_value), dq_all = lax.scan(sub_step, (zero_acc, zero_acc), (q_grp, do_grp, row_stats, firsts), reverse=True)
        return dq_all, d_key, d_value

    return jax.shard_map(local_backward, mesh=mesh, in_specs=(q_spec, q_spec, q_spec, lse_spec, kv_spec, kv_spec, P()), out_specs=(q_spec, kv_spec, kv_spec), check_vma=False)
```

profile of v0, /device:TPU:22, one launch (start us, length us, event | category | flops | bytes accessed | tf_op | source)
XLA Modules:
  0.0 2290.6 jit_solution(2579490750036569639)
XLA Ops:
  19.4 2261.4 %while.19 = (s32[]{:T(128)}, f32[640,2,128]{0,2,1:T(8,128)S(1)}, f32[640,2,128]{0,2,1:T(8,128)}, bf16[16,32,8,128]{3,2,1,0:T(8,128)(2,1)}, bf16[16,32,2,4,128]{4...) while((s32[]{:T(128)}, f32[640,2,128]{0,2,1:T(8,128)S(1)}, ...), condition=%wide.region_2.3_spmd.clone, body=%wide.region_0.2_spmd.clone.sunk | while | flops 3384017920 | bytes 102957656 | solution.py:50
  68.2 29.1 %all-gather.17.cloned.1.call-done = bf16[1,512,2,4,128]{4,1,3,2,0:T(8,128)(2,1)} async-done(((bf16[1,32,2,4,128]{4,1,3,2,0:T(8,128)(2,1)}), bf16[1,512,2,4,128]{4,1,3,2,0:T(8,128)(2,1)}) %all-gather.17.cloned.1.call-update) | async-done | bytes 1048592 | tf_op jit(solution)/shard_map/while/body/eval_jaxpr/all_gather | solution.py:34
  119.1 45.1 %reduce-scatter.2.cloned.1.call-done = f32[32,2,4,128]{3,0,2,1:T(8,128)} async-done(((f32[512,2,4,128]{3,0,2,1:T(8,128)}), f32[32,2,4,128]{3,0,2,1:T(8,128)}) %reduce-scatter.2.cloned.1.call-update) | async-done | bytes 131088 | tf_op jit(solution)/shard_map/while/body/eval_jaxpr/reduce_scatter | solution.py:46
  209.3 28.8 %all-gather.17.cloned.1.call-done = bf16[1,512,2,4,128]{4,1,3,2,0:T(8,128)(2,1)} async-done(((bf16[1,32,2,4,128]{4,1,3,2,0:T(8,128)(2,1)}), bf16[1,512,2,4,128]{4,1,3,2,0:T(8,128)(2,1)}) %all-gather.17.cloned.1.call-update) | async-done | bytes 1048592 | tf_op jit(solution)/shard_map/while/body/eval_jaxpr/all_gather | solution.py:34
  260.0 44.9 %reduce-scatter.2.cloned.1.call-done = f32[32,2,4,128]{3,0,2,1:T(8,128)} async-done(((f32[512,2,4,128]{3,0,2,1:T(8,128)}), f32[32,2,4,128]{3,0,2,1:T(8,128)}) %reduce-scatter.2.cloned.1.call-update) | async-done | bytes 131088 | tf_op jit(solution)/shard_map/while/body/eval_jaxpr/reduce_scatter | solution.py:46
  401.2 44.9 %reduce-scatter.2.cloned.1.call-done = f32[32,2,4,128]{3,0,2,1:T(8,128)} async-done(((f32[512,2,4,128]{3,0,2,1:T(8,128)}), f32[32,2,4,128]{3,0,2,1:T(8,128)}) %reduce-scatter.2.cloned.1.call-update) | async-done | bytes 131088 | tf_op jit(solution)/shard_map/while/body/eval_jaxpr/reduce_scatter | solution.py:46
  491.3 28.9 %all-gather.17.cloned.1.call-done = bf16[1,512,2,4,128]{4,1,3,2,0:T(8,128)(2,1)} async-done(((bf16[1,32,2,4,128]{4,1,3,2,0:T(8,128)(2,1)}), bf16[1,512,2,4,128]{4,1,3,2,0:T(8,128)(2,1)}) %all-gather.17.cloned.1.call-update) | async-done | bytes 1048592 | tf_op jit(solution)/shard_map/while/body/eval_jaxpr/all_gather | solution.py:34
  542.1 44.9 %reduce-scatter.2.cloned.1.call-done = f32[32,2,4,128]{3,0,2,1:T(8,128)} async-done(((f32[512,2,4,128]{3,0,2,1:T(8,128)}), f32[32,2,4,128]{3,0,2,1:T(8,128)}) %reduce-scatter.2.cloned.1.call-update) | async-done | bytes 131088 | tf_op jit(solution)/shard_map/while/body/eval_jaxpr/reduce_scatter | solution.py:46
  683.1 44.9 %reduce-scatter.2.cloned.1.call-done = f32[32,2,4,128]{3,0,2,1:T(8,128)} async-done(((f32[512,2,4,128]{3,0,2,1:T(8,128)}), f32[32,2,4,128]{3,0,2,1:T(8,128)}) %reduce-scatter.2.cloned.1.call-update) | async-done | bytes 131088 | tf_op jit(solution)/shard_map/while/body/eval_jaxpr/reduce_scatter | solution.py:46
  773.2 28.8 %all-gather.17.cloned.1.call-done = bf16[1,512,2,4,128]{4,1,3,2,0:T(8,128)(2,1)} async-done(((bf16[1,32,2,4,128]{4,1,3,2,0:T(8,128)(2,1)}), bf16[1,512,2,4,128]{4,1,3,2,0:T(8,128)(2,1)}) %all-gather.17.cloned.1.call-update) | async-done | bytes 1048592 | tf_op jit(solution)/shard_map/while/body/eval_jaxpr/all_gather | solution.py:34
  823.9 44.9 %reduce-scatter.2.cloned.1.call-done = f32[32,2,4,128]{3,0,2,1:T(8,128)} async-done(((f32[512,2,4,128]{3,0,2,1:T(8,128)}), f32[32,2,4,128]{3,0,2,1:T(8,128)}) %reduce-scatter.2.cloned.1.call-update) | async-done | bytes 131088 | tf_op jit(solution)/shard_map/while/body/eval_jaxpr/reduce_scatter | solution.py:46
  964.9 44.9 %reduce-scatter.2.cloned.1.call-done = f32[32,2,4,128]{3,0,2,1:T(8,128)} async-done(((f32[512,2,4,128]{3,0,2,1:T(8,128)}), f32[32,2,4,128]{3,0,2,1:T(8,128)}) %reduce-scatter.2.cloned.1.call-update) | async-done | bytes 131088 | tf_op jit(solution)/shard_map/while/body/eval_jaxpr/reduce_scatter | solution.py:46
  1106.0 44.9 %reduce-scatter.2.cloned.1.call-done = f32[32,2,4,128]{3,0,2,1:T(8,128)} async-done(((f32[512,2,4,128]{3,0,2,1:T(8,128)}), f32[32,2,4,128]{3,0,2,1:T(8,128)}) %reduce-scatter.2.cloned.1.call-update) | async-done | bytes 131088 | tf_op jit(solution)/shard_map/while/body/eval_jaxpr/reduce_scatter | solution.py:46
  1247.1 44.9 %reduce-scatter.2.cloned.1.call-done = f32[32,2,4,128]{3,0,2,1:T(8,128)} async-done(((f32[512,2,4,128]{3,0,2,1:T(8,128)}), f32[32,2,4,128]{3,0,2,1:T(8,128)}) %reduce-scatter.2.cloned.1.call-update) | async-done | bytes 131088 | tf_op jit(solution)/shard_map/while/body/eval_jaxpr/reduce_scatter | solution.py:46
  1388.3 44.9 %reduce-scatter.2.cloned.1.call-done = f32[32,2,4,128]{3,0,2,1:T(8,128)} async-done(((f32[512,2,4,128]{3,0,2,1:T(8,128)}), f32[32,2,4,128]{3,0,2,1:T(8,128)}) %reduce-scatter.2.cloned.1.call-update) | async-done | bytes 131088 | tf_op jit(solution)/shard_map/while/body/eval_jaxpr/reduce_scatter | solution.py:46
  1529.5 44.9 %reduce-scatter.2.cloned.1.call-done = f32[32,2,4,128]{3,0,2,1:T(8,128)} async-done(((f32[512,2,4,128]{3,0,2,1:T(8,128)}), f32[32,2,4,128]{3,0,2,1:T(8,128)}) %reduce-scatter.2.cloned.1.call-update) | async-done | bytes 131088 | tf_op jit(solution)/shard_map/while/body/eval_jaxpr/reduce_scatter | solution.py:46
  1670.7 44.9 %reduce-scatter.2.cloned.1.call-done = f32[32,2,4,128]{3,0,2,1:T(8,128)} async-done(((f32[512,2,4,128]{3,0,2,1:T(8,128)}), f32[32,2,4,128]{3,0,2,1:T(8,128)}) %reduce-scatter.2.cloned.1.call-update) | async-done | bytes 131088 | tf_op jit(solution)/shard_map/while/body/eval_jaxpr/reduce_scatter | solution.py:46
  1760.7 28.8 %all-gather.17.cloned.1.call-done = bf16[1,512,2,4,128]{4,1,3,2,0:T(8,128)(2,1)} async-done(((bf16[1,32,2,4,128]{4,1,3,2,0:T(8,128)(2,1)}), bf16[1,512,2,4,128]{4,1,3,2,0:T(8,128)(2,1)}) %all-gather.17.cloned.1.call-update) | async-done | bytes 1048592 | tf_op jit(solution)/shard_map/while/body/eval_jaxpr/all_gather | solution.py:34
  1811.4 44.9 %reduce-scatter.2.cloned.1.call-done = f32[32,2,4,128]{3,0,2,1:T(8,128)} async-done(((f32[512,2,4,128]{3,0,2,1:T(8,128)}), f32[32,2,4,128]{3,0,2,1:T(8,128)}) %reduce-scatter.2.cloned.1.call-update) | async-done | bytes 131088 | tf_op jit(solution)/shard_map/while/body/eval_jaxpr/reduce_scatter | solution.py:46
  1952.8 44.9 %reduce-scatter.2.cloned.1.call-done = f32[32,2,4,128]{3,0,2,1:T(8,128)} async-done(((f32[512,2,4,128]{3,0,2,1:T(8,128)}), f32[32,2,4,128]{3,0,2,1:T(8,128)}) %reduce-scatter.2.cloned.1.call-update) | async-done | bytes 131088 | tf_op jit(solution)/shard_map/while/body/eval_jaxpr/reduce_scatter | solution.py:46
  2042.8 28.8 %all-gather.17.cloned.1.call-done = bf16[1,512,2,4,128]{4,1,3,2,0:T(8,128)(2,1)} async-done(((bf16[1,32,2,4,128]{4,1,3,2,0:T(8,128)(2,1)}), bf16[1,512,2,4,128]{4,1,3,2,0:T(8,128)(2,1)}) %all-gather.17.cloned.1.call-update) | async-done | bytes 1048592 | tf_op jit(solution)/shard_map/while/body/eval_jaxpr/all_gather | solution.py:34
  2093.6 44.9 %reduce-scatter.2.cloned.1.call-done = f32[32,2,4,128]{3,0,2,1:T(8,128)} async-done(((f32[512,2,4,128]{3,0,2,1:T(8,128)}), f32[32,2,4,128]{3,0,2,1:T(8,128)}) %reduce-scatter.2.cloned.1.call-update) | async-done | bytes 131088 | tf_op jit(solution)/shard_map/while/body/eval_jaxpr/reduce_scatter | solution.py:46
  2183.6 28.8 %all-gather.17.cloned.1.call-done = bf16[1,512,2,4,128]{4,1,3,2,0:T(8,128)(2,1)} async-done(((bf16[1,32,2,4,128]{4,1,3,2,0:T(8,128)(2,1)}), bf16[1,512,2,4,128]{4,1,3,2,0:T(8,128)(2,1)}) %all-gather.17.cloned.1.call-update) | async-done | bytes 1048592 | tf_op jit(solution)/shard_map/while/body/eval_jaxpr/all_gather | solution.py:34
  2234.3 44.9 %reduce-scatter.2.cloned.1.call-done = f32[32,2,4,128]{3,0,2,1:T(8,128)} async-done(((f32[512,2,4,128]{3,0,2,1:T(8,128)}), f32[32,2,4,128]{3,0,2,1:T(8,128)}) %reduce-scatter.2.cloned.1.call-update) | async-done | bytes 131088 | tf_op jit(solution)/shard_map/while/body/eval_jaxpr/reduce_scatter | solution.py:46
  (715 shorter events, 1322.9 us)
Async XLA Ops:
  21.0 76.4 %all-gather.17.cloned.1.call-start = ((), (), s32[]{:S(2)}) async-start(), calls=%async_computation.2 | async-start | bytes 1114112 | tf_op jit(solution)/shard_map/while/body/eval_jaxpr/all_gather | solution.py:34
  21.8 142.3 %reduce-scatter.2.cloned.1.call-start = ((), (), s32[]{:S(2)}) async-start(), calls=%async_computation.3 | async-start | bytes 2228224 | tf_op jit(solution)/shard_map/while/body/eval_jaxpr/reduce_scatter | solution.py:46
  168.1 136.8 %reduce-scatter.2.cloned.1.call-start = ((), (), s32[]{:S(2)}) async-start(), calls=%async_computation.3 | async-start | bytes 2228224 | tf_op jit(solution)/shard_map/while/body/eval_jaxpr/reduce_scatter | solution.py:46
  308.1 71.2 %all-gather.17.cloned.1.call-start = ((), (), s32[]{:S(2)}) async-start(), calls=%async_computation.2 | async-start | bytes 1114112 | tf_op jit(solution)/shard_map/while/body/eval_jaxpr/all_gather | solution.py:34
  309.0 137.1 %reduce-scatter.2.cloned.1.call-start = ((), (), s32[]{:S(2)}) async-start(), calls=%async_computation.3 | async-start | bytes 2228224 | tf_op jit(solution)/shard_map/while/body/eval_jaxpr/reduce_scatter | solution.py:46
  450.1 136.9 %reduce-scatter.2.cloned.1.call-start = ((), (), s32[]{:S(2)}) async-start(), calls=%async_computation.3 | async-start | bytes 2228224 | tf_op jit(solution)/shard_map/while/body/eval_jaxpr/reduce_scatter | solution.py:46
  591.0 137.0 %reduce-scatter.2.cloned.1.call-start = ((), (), s32[]{:S(2)}) async-start(), calls=%async_computation.3 | async-start | bytes 2228224 | tf_op jit(solution)/shard_map/while/body/eval_jaxpr/reduce_scatter | solution.py:46
  732.0 136.8 %reduce-scatter.2.cloned.1.call-start = ((), (), s32[]{:S(2)}) async-start(), calls=%async_computation.3 | async-start | bytes 2228224 | tf_op jit(solution)/shard_map/while/body/eval_jaxpr/reduce_scatter | solution.py:46
  872.8 137.0 %reduce-scatter.2.cloned.1.call-start = ((), (), s32[]{:S(2)}) async-start(), calls=%async_computation.3 | async-start | bytes 2228224 | tf_op jit(solution)/shard_map/while/body/eval_jaxpr/reduce_scatter | solution.py:46
  1013.0 71.2 %all-gather.17.cloned.1.call-start = ((), (), s32[]{:S(2)}) async-start(), calls=%async_computation.2 | async-start | bytes 1114112 | tf_op jit(solution)/shard_map/while/body/eval_jaxpr/all_gather | solution.py:34
  1013.8 137.1 %reduce-scatter.2.cloned.1.call-start = ((), (), s32[]{:S(2)}) async-start(), calls=%async_computation.3 | async-start | bytes 2228224 | tf_op jit(solution)/shard_map/while/body/eval_jaxpr/reduce_scatter | solution.py:46
  1154.2 71.0 %all-gather.17.cloned.1.call-start = ((), (), s32[]{:S(2)}) async-start(), calls=%async_computation.2 | async-start | bytes 1114112 | tf_op jit(solution)/shard_map/while/body/eval_jaxpr/all_gather | solution.py:34
  1154.9 137.0 %reduce-scatter.2.cloned.1.call-start = ((), (), s32[]{:S(2)}) async-start(), calls=%async_computation.3 | async-start | bytes 2228224 | tf_op jit(solution)/shard_map/while/body/eval_jaxpr/reduce_scatter | solution.py:46
  1295.2 71.2 %all-gather.17.cloned.1.call-start = ((), (), s32[]{:S(2)}) async-start(), calls=%async_computation.2 | async-start | bytes 1114112 | tf_op jit(solution)/shard_map/while/body/eval_jaxpr/all_gather | solution.py:34
  1296.0 137.2 %reduce-scatter.2.cloned.1.call-start = ((), (), s32[]{:S(2)}) async-start(), calls=%async_computation.3 | async-start | bytes 2228224 | tf_op jit(solution)/shard_map/while/body/eval_jaxpr/reduce_scatter | solution.py:46
  1436.4 71.2 %all-gather.17.cloned.1.call-start = ((), (), s32[]{:S(2)}) async-start(), calls=%async_computation.2 | async-start | bytes 1114112 | tf_op jit(solution)/shard_map/while/body/eval_jaxpr/all_gather | solution.py:34
  1437.2 137.2 %reduce-scatter.2.cloned.1.call-start = ((), (), s32[]{:S(2)}) async-start(), calls=%async_computation.3 | async-start | bytes 2228224 | tf_op jit(solution)/shard_map/while/body/eval_jaxpr/reduce_scatter | solution.py:46
  1577.6 71.2 %all-gather.17.cloned.1.call-start = ((), (), s32[]{:S(2)}) async-start(), calls=%async_computation.2 | async-start | bytes 1114112 | tf_op jit(solution)/shard_map/while/body/eval_jaxpr/all_gather | solution.py:34
  1578.4 137.1 %reduce-scatter.2.cloned.1.call-start = ((), (), s32[]{:S(2)}) async-start(), calls=%async_computation.3 | async-start | bytes 2228224 | tf_op jit(solution)/shard_map/while/body/eval_jaxpr/reduce_scatter | solution.py:46
  1719.6 136.8 %reduce-scatter.2.cloned.1.call-start = ((), (), s32[]{:S(2)}) async-start(), calls=%async_computation.3 | async-start | bytes 2228224 | tf_op jit(solution)/shard_map/while/body/eval_jaxpr/reduce_scatter | solution.py:46
  1859.6 71.3 %all-gather.17.cloned.1.call-start = ((), (), s32[]{:S(2)}) async-start(), calls=%async_computation.2 | async-start | bytes 1114112 | tf_op jit(solution)/shard_map/while/body/eval_jaxpr/all_gather | solution.py:34
  1860.4 137.3 %reduce-scatter.2.cloned.1.call-start = ((), (), s32[]{:S(2)}) async-start(), calls=%async_computation.3 | async-start | bytes 2228224 | tf_op jit(solution)/shard_map/while/body/eval_jaxpr/reduce_scatter | solution.py:46
  2001.7 136.8 %reduce-scatter.2.cloned.1.call-start = ((), (), s32[]{:S(2)}) async-start(), calls=%async_computation.3 | async-start | bytes 2228224 | tf_op jit(solution)/shard_map/while/body/eval_jaxpr/reduce_scatter | solution.py:46
  2142.5 136.8 %reduce-scatter.2.cloned.1.call-start = ((), (), s32[]{:S(2)}) async-start(), calls=%async_computation.3 | async-start | bytes 2228224 | tf_op jit(solution)/shard_map/while/body/eval_jaxpr/reduce_scatter | solution.py:46
  (153 other events, 4997.0 us)
Sparse Core Ops, SparseCore 0:
  22.5 38.9 all-gather.14
  63.1 34.2 all-gather.16
  109.0 55.1 reduce-scatter.1
  249.7 55.1 reduce-scatter.1
  309.6 34.1 all-gather.14
  390.9 55.1 reduce-scatter.1
  531.8 55.1 reduce-scatter.1
  672.8 55.1 reduce-scatter.1
  813.6 55.1 reduce-scatter.1
  954.6 55.1 reduce-scatter.1
  1014.5 34.2 all-gather.14
  1095.7 55.1 reduce-scatter.1
  1155.6 34.2 all-gather.14
  1236.8 55.1 reduce-scatter.1
  1296.6 34.2 all-gather.14
  1378.0 55.1 reduce-scatter.1
  1437.9 34.2 all-gather.14
  1519.2 55.1 reduce-scatter.1
  1660.4 55.1 reduce-scatter.1
  1801.1 55.1 reduce-scatter.1
  1861.0 34.3 all-gather.14
  1942.5 55.1 reduce-scatter.1
  2083.3 55.1 reduce-scatter.1
  2224.0 55.1 reduce-scatter.1
  (24 shorter events, 813.4 us)
where the time goes:
time: 2290 us
  waiting for transfers between devices  1340 us (59%)
  matrix products  418 us (18%)
  blocking collectives  309 us (13%)
  local copies, waits for them, and re-layouts  140 us (6%)
  loops' own time  33.1 us (1%)
  other arithmetic  32.3 us (1%)
    reduce_scatter x16, waiting for transfers between devices, sub_step(): dq_sum = lax.psum_scatter(dq_part, 'cp', scatter_dimension=0, tiled=True)  719 us
    all_gather x16, waiting for transfers between devices, sub_step(): do_all = lax.all_gather(do_loc, 'cp', axis=0, tiled=True)  460 us
    all_gather x16, blocking collectives, sub_step(): stats_all = lax.all_gather(stats_loc, 'cp', axis=0, tiled=True)  309 us
    all_gather x16, waiting for transfers between devices, sub_step(): q_all = lax.all_gather(q_loc, 'cp', axis=0, tiled=True)  159 us
    dot_general x16, matrix products, sub_step(): jnp.einsum('qhgd,khd->qhgk', q_all, key_act, preferred_element_type=jnp.f...  109 us
    dot_general x16, matrix products, sub_step(): jnp.einsum('qhgk,qhgd->khd', p_full.astype(jnp.bfloat16), do_all, preferr...  104 us
    dot_general x16, matrix products, sub_step(): jnp.einsum('qhgd,khd->qhgk', do_all, value_act, preferred_element_type=jn...  98.6 us
    dot_general x16, matrix products, sub_step(): jnp.einsum('qhgk,qhgd->khd', d_score, q_all, preferred_element_type=jnp.f...  61.2 us
  transfers between devices with their start and end apart: 48, of which 48 were waited for; matrix products, arithmetic and copies ran while one was open for 15% of the time, Pallas kernels for 0%

commit v1 on v0

v1 whole, which is shorter than its diff:
```python
import functools
import math

import jax
import jax.numpy as jnp
from jax import lax
from jax.experimental import pallas as pl
from jax.experimental.pallas import tpu as pltpu
from jax.sharding import PartitionSpec as P

MESH = pl.DeviceIdType.MESH
CORES = 2
F32 = jnp.float32
BF16 = jnp.bfloat16


def ring_kernel(cp_size, sub_start, local_len, scale, kv_in, q_in, qt_in, do_in, dot_in, st_in, dq_out, dkv_out,
                kvb, acc, rsb, qn, qt, don, dot, st, dqa, dqr, dqo,
                ag_send, ag_recv, rs_send, rs_recv, x_send, x_recv, loc_sem, out_sem):
    n_chip = cp_size // CORES
    n_hop = n_chip - 1
    n_kv, n_sub, rows = q_in.shape[0], q_in.shape[1], q_in.shape[2]
    key_tile = kv_in.shape[2]
    head_dim = kv_in.shape[3] // 2
    span = local_len * CORES
    sub_len = local_len * cp_size
    keys_local = 2 * key_tile
    own = 2 * n_hop

    me = lax.axis_index('cp')
    chip, core = me // CORES, lax.rem(me, CORES)
    right = lax.rem(me + CORES, cp_size)
    left = lax.rem(me + cp_size - CORES, cp_size)
    sibling = me + 1 - 2 * core
    nbr = (right, left)

    barrier = pltpu.get_barrier_semaphore()
    for peer in (right, left, sibling):
        pl.semaphore_signal(barrier, inc=1, device_id={'cp': peer}, device_id_type=MESH)
    pl.semaphore_wait(barrier, 3)

    def remote(src, dst, send, recv, peer):
        return pltpu.make_async_remote_copy(src_ref=src, dst_ref=dst, send_sem=send, recv_sem=recv,
                                            device_id={'cp': peer}, device_id_type=MESH)

    def half_of(way, k):
        return (k + way) % 2

    def gather(way, j):
        src = kv_in.at[half_of(way, j)] if j < 2 else kvb.at[way * n_hop + j - 2]
        i = way * n_hop + j
        return remote(src, kvb.at[i], ag_send.at[i], ag_recv.at[i], nbr[way])

    def reduce_copy(way, k):
        i = way * n_hop + k
        return remote(acc.at[i], rsb.at[i], rs_send.at[i], rs_recv.at[i], nbr[1 - way])

    pairs = ((q_in, qn), (qt_in, qt), (do_in, don), (dot_in, dot), (st_in, st))

    def part_of(ref, which):
        cut = pl.ds(which * rows, rows)
        return ref.at[:, :, cut, :] if ref.shape[2] == CORES * rows and ref.shape[3] == head_dim else ref.at[:, :, :, cut]

    share = [remote(a, part_of(b, 1), x_send.at[i], x_recv.at[i], sibling) for i, (a, b) in enumerate(pairs)]
    local = [pltpu.make_async_copy(a, part_of(b, 0), loc_sem.at[i]) for i, (a, b) in enumerate(pairs)]
    local.append(pltpu.make_async_copy(kv_in, kvb.at[pl.ds(own, 2)], loc_sem.at[len(pairs)]))
    for j in range(2):
        for way in range(2):
            gather(way, j).start()
    for c in share + local:
        c.start()

    @pl.loop(0, n_kv * n_sub)
    def _(i):
        dqa[i // n_sub, lax.rem(i, n_sub)] = jnp.zeros(dqa.shape[2:], F32)

    for c in local:
        c.wait()
    for c in share:
        c.wait()

    exp_scale = scale * math.log2(math.e)
    k_iota = lax.broadcasted_iota(jnp.int32, (key_tile, CORES * rows), 0).astype(F32)

    def chunk(slot, key_chip, half, head):
        pos0 = (key_chip * CORES + core) * keys_local + half * key_tile
        t = pos0 - sub_start - span * chip - span + sub_len
        s_lo = jnp.minimum(jnp.maximum(t, 0) // sub_len, n_sub)
        pos_f = pos0.astype(F32)
        k = kvb[slot, head, :, :head_dim]
        v = kvb[slot, head, :, head_dim:]
        acc[slot, head] = jnp.zeros(acc.shape[2:], F32)

        @pl.loop(s_lo, n_sub)
        def _(s):
            lse, delta = st[head, s, 0:1, :], st[head, s, 1:2, :]
            lo, hi = st[head, s, 2:3, :] - pos_f, st[head, s, 3:4, :] - pos_f
            s_t = jnp.dot(k, qt[head, s], preferred_element_type=F32)
            dp_t = jnp.dot(v, dot[head, s], preferred_element_type=F32)
            ok = (k_iota >= lo) & (k_iota <= hi)
            p = jnp.where(ok, jnp.exp2(s_t * exp_scale - lse), 0.0)
            ds = (p * (dp_t - delta)).astype(BF16)
            acc[slot, head, :, head_dim:] += jnp.dot(p.astype(BF16), don[head, s], preferred_element_type=F32)
            acc[slot, head, :, :head_dim] += jnp.dot(ds, qn[head, s], preferred_element_type=F32)
            dqa[head, s] += lax.dot_general(ds, k, (((0,), (0,)), ((), ())), preferred_element_type=F32)

    def unit(way, k):
        if way is None:
            slot, key_chip, half = own + k, chip, k
        else:
            hop = k // 2 + 1
            slot, half = way * n_hop + k, half_of(way, k)
            key_chip = lax.rem(chip + (hop if way else n_chip - hop), n_chip)
        for head in range(n_kv):
            chunk(slot, key_chip, half, head)

    def event(k):
        for way in range(2):
            gather(way, k).wait_recv()
            if k + 2 < n_hop:
                gather(way, k + 2).start()

    def add(dst, src):
        steps = n_kv * 4
        cut = key_tile // 4

        @pl.loop(0, steps)
        def _(i):
            h, r = i // 4, pl.ds(pl.multiple_of(lax.rem(i, 4) * cut, 8), cut)
            acc[dst, h, r, :] += rsb[src, h, r, :]

    units = [(None, 0), (None, 1)] + [(way, k) for k in range(n_hop) for way in range(2)]
    done = units[:n_hop]
    for k in range(n_hop):
        unit(*done[k])
        event(k)
    for k in reversed(range(n_hop)):
        for way in range(2):
            if (way, k) not in done:
                unit(way, k)
            if k + 2 < n_hop:
                reduce_copy(way, k + 2).wait_recv()
                add(way * n_hop + k, way * n_hop + k + 2)
            reduce_copy(way, k).start()
    for u in ((None, 0), (None, 1)):
        if u not in done:
            unit(*u)
    swap = remote(part_of(dqa, 1), dqr, x_send.at[len(pairs)], x_recv.at[len(pairs)], sibling)
    swap.start()
    swap.wait_recv()

    @pl.loop(0, n_kv * n_sub)
    def _(i):
        h, s = i // n_sub, lax.rem(i, n_sub)
        dqo[h, s] = ((dqa[h, s, :rows, :] + dqr[h, s]) * scale).astype(BF16)

    put_dq = pltpu.make_async_copy(dqo, dq_out, out_sem.at[0])
    put_dq.start()
    for k in reversed(range(min(2, n_hop))):
        for way in range(2):
            reduce_copy(way, k).wait_recv()
            add(own + half_of(way, k), way * n_hop + k)

    @pl.loop(0, 2 * n_kv)
    def _(i):
        half, h = i // n_kv, lax.rem(i, n_kv)
        acc[own + half, h, :, :head_dim] = acc[own + half, h, :, :head_dim] * scale

    put_kv = pltpu.make_async_copy(acc.at[pl.ds(own, 2)], dkv_out, out_sem.at[1])
    put_kv.start()
    swap.wait_send()
    for way in range(2):
        for j in range(n_hop):
            gather(way, j).wait_send()
            reduce_copy(way, j).wait_send()
    put_dq.wait()
    put_kv.wait()


def solution(mesh):
    cp_size = mesh.shape['cp']
    q_spec = P(None, 'cp', 'tp', None)
    lse_spec = P(None, 'cp', 'tp')
    kv_spec = P('cp', 'tp', None)

    def local_backward(query, out_act, out_grad, row_lse, key_act, value_act, doc_ids):
        n_sub, local_len, n_heads, head_dim = query.shape
        keys_local, n_kv = key_act.shape[0], key_act.shape[1]
        group = n_heads // n_kv
        sub_len = local_len * cp_size
        sub_start = keys_local * cp_size - n_sub * sub_len
        scale = head_dim ** -0.5
        rows = local_len * group
        half = keys_local // 2
        n_hop = cp_size // CORES - 1
        n_slot = 2 * n_hop + 2
        me = lax.axis_index('cp')

        def by_head(x):
            x = x.reshape((n_sub, local_len, n_kv, group) + x.shape[3:])
            x = jnp.moveaxis(x, 2, 0)
            return x.reshape((n_kv, n_sub, rows) + x.shape[4:])

        delta = jnp.einsum('sqhd,sqhd->sqh', out_grad, out_act, preferred_element_type=F32)
        q_doc = lax.dynamic_slice_in_dim(doc_ids[sub_start:].reshape(n_sub, sub_len), me * local_len, local_len, axis=1)
        q_first = jnp.sum((doc_ids[None, None, :] < q_doc[:, :, None]).astype(F32), axis=-1)
        q_pos = (sub_start + me * local_len + jnp.arange(n_sub)[:, None] * sub_len + jnp.arange(local_len)[None, :]).astype(F32)
        wide = lambda x: jnp.broadcast_to(jnp.repeat(x, group, axis=1)[None], (n_kv, n_sub, rows))
        lines = [by_head(row_lse) * math.log2(math.e), by_head(delta), wide(q_first), wide(q_pos)]
        stats = jnp.stack(lines + [jnp.zeros_like(lines[0])] * 4, axis=2)
        qn, don = by_head(query), by_head(out_grad)
        cut = lambda x: jnp.transpose(x.reshape(2, half, n_kv, head_dim), (0, 2, 1, 3))
        kv = jnp.concatenate([cut(key_act), cut(value_act)], axis=-1)
        flops = 2 * 5 * n_kv * n_sub * 2 * rows * head_dim * keys_local * n_hop
        hbm = pl.BlockSpec(memory_space=pl.ANY)
        dma = pltpu.SemaphoreType.DMA
        dq, dkv = pl.pallas_call(
            functools.partial(ring_kernel, cp_size, sub_start, local_len, scale),
            name='ring_backward',
            out_shape=(jax.ShapeDtypeStruct((n_kv, n_sub, rows, head_dim), BF16),
                       jax.ShapeDtypeStruct((2, n_kv, half, 2 * head_dim), F32)),
            in_specs=[hbm] * 6,
            out_specs=(hbm, hbm),
            scratch_shapes=[
                pltpu.VMEM((n_slot, n_kv, half, 2 * head_dim), BF16),
                pltpu.VMEM((n_slot, n_kv, half, 2 * head_dim), F32),
                pltpu.VMEM((2 * n_hop, n_kv, half, 2 * head_dim), F32),
                pltpu.VMEM((n_kv, n_sub, CORES * rows, head_dim), BF16),
                pltpu.VMEM((n_kv, n_sub, head_dim, CORES * rows), BF16),
                pltpu.VMEM((n_kv, n_sub, CORES * rows, head_dim), BF16),
                pltpu.VMEM((n_kv, n_sub, head_dim, CORES * rows), BF16),
                pltpu.VMEM((n_kv, n_sub, 8, CORES * rows), F32),
                pltpu.VMEM((n_kv, n_sub, CORES * rows, head_dim), F32),
                pltpu.VMEM((n_kv, n_sub, rows, head_dim), F32),
                pltpu.VMEM((n_kv, n_sub, rows, head_dim), BF16),
                dma((2 * n_hop,)), dma((2 * n_hop,)), dma((2 * n_hop,)), dma((2 * n_hop,)),
                dma((6,)), dma((6,)), dma((6,)), dma((2,)),
            ],
            compiler_params=pltpu.CompilerParams(collective_id=0, has_side_effects=True, vmem_limit_bytes=62 * 1024 * 1024),
            cost_estimate=pl.CostEstimate(flops=flops, bytes_accessed=30 * 2 ** 20, transcendentals=0),
        )(kv, qn, jnp.swapaxes(qn, 2, 3), don, jnp.swapaxes(don, 2, 3), stats)
        dq = jnp.moveaxis(dq.reshape(n_kv, n_sub, local_len, group, head_dim), 0, 2).reshape(query.shape)
        dkv = jnp.transpose(dkv, (0, 2, 1, 3)).reshape(keys_local, n_kv, 2 * head_dim)
        return dq, dkv[..., :head_dim], dkv[..., head_dim:]

    return jax.shard_map(local_backward, mesh=mesh, in_specs=(q_spec, q_spec, q_spec, lse_spec, kv_spec, kv_spec, P()),
                         out_specs=(q_spec, kv_spec, kv_spec), check_vma=False)
```

time: 2290 us -> 261 us (0.11)
  waiting for transfers between devices: 1340 us -> 0 us
  matrix products: 418 us -> 0 us
  blocking collectives: 309 us -> 0 us
  Pallas kernels: 0 us -> 236 us
  local copies, waits for them, and re-layouts: 140 us -> 16.3 us
  loops' own time: 33.1 us -> 0 us
  other arithmetic: 32.3 us -> 6.72 us
    reduce_scatter x16 -> x0, waiting for transfers between devices: 719 us -> none  [sub_step(): dq_sum = lax.psum_scatter(dq_part, 'cp', scatter_dimension=0, tiled=True)]
    all_gather x32 -> x0, waiting for transfers between devices: 619 us -> none  [the longest x16 460 us: sub_step(): do_all = lax.all_gather(do_loc, 'cp', axis=0, tiled=True)]
    dot_general x80 -> x0, matrix products: 418 us -> none  [the longest x16 109 us: sub_step(): jnp.einsum('qhgd,khd->qhgk', q_all, key_act, preferred_element_type=jnp.f...]
    all_gather x16 -> x0, blocking collectives: 309 us -> none  [sub_step(): stats_all = lax.all_gather(stats_loc, 'cp', axis=0, tiled=True)]
    pallas_call x0 -> x1, Pallas kernels: none -> 236 us  [local_backward(): pl.pallas_call(functools.partial(ring_kernel, cp_size, sub_start, local_l...]
    dynamic_slice x97 -> x1, local copies, waits for them, and re-layouts: 59.9 us -> 0.08 us  [local_backward(): lax.dynamic_slice_in_dim(doc_ids[sub_start:].reshape(n_sub, sub_len), me...]
    while x256 -> x0, local copies, waits for them, and re-layouts: 38.2 us -> none
    another operation x1 -> x0, loops' own time: 33.1 us -> none  [local_backward(): lax.scan(sub_step, (zero_acc, zero_acc), (q_grp, do_grp, row_stats, first...]
  transfers between devices with their start and end apart: 48 -> 0, of which waited for: 48 -> 0; matrix products, arithmetic and copies ran while one was open for 15% -> 0% of each run, Pallas kernels for 0% -> 0%
where the time goes in v1:
time: 261 us; the launch traced here: 260 us
  Pallas kernels  236 us (90%)
  local copies, waits for them, and re-layouts  16.3 us (6%)
  other arithmetic  6.72 us (3%)
    pallas_call x1, Pallas kernels, local_backward(): pl.pallas_call(functools.partial(ring_kernel, cp_size, sub_start, local_l...  236 us
    reshape x4, local copies, waits for them, and re-layouts, by_head(): return x.reshape((n_kv, n_sub, rows) + x.shape[4:])  5.89 us

profile of v1, /device:TPU:22, one launch (start us, length us, event | category | flops | bytes accessed | tf_op | source)
XLA Modules:
  0.0 260.2 jit_solution(16029874711654466822)
XLA Ops:
  0.7 0.8 slice.19
  1.6 3.0 %convert_reduce_fusion = f32[16,32]{1,0:T(8,128)S(1)} fusion(s32[16,32]{1,0:T(8,128)S(1)} %constant_dynamic-slice_fusion, s32[10240]{0:T(1024)} %param.13), kind=kLoop, calls=%fused_computation | loop fusion | flops 15728128 | bytes 45056 | tf_op jit(solution)/shard_map/reduce_sum | solution.py:206
  4.9 0.8 broadcast_multiply_fusion
  5.8 0.1 copy.66
  6.0 1.9 fusion
  7.9 0.1 copy.83
  8.0 0.1 copy.67
  8.2 0.8 stack.8.st_in
  9.0 0.1 copy_bitcast_fusion
  9.1 0.9 pad_maximum_fusion.kv_in
  10.0 0.5 copy-done.2
  10.5 0.2 copy.60
  10.7 0.7 copy.61
  11.4 1.2 copy.73.q_in
  12.7 1.7 copy.62
  14.4 0.2 copy.63
  14.6 0.7 copy.64
  15.3 1.2 copy.74.do_in
  16.6 1.7 copy.65
  18.3 236.4 %ring_backward.1 = (bf16[2,16,128,128]{3,2,1,0:T(8,128)(2,1)}, f32[2,2,320,256]{3,2,1,0:T(8,128)}) custom-call(bf16[2,2,320,256]{3,2,1,0:T(8,128)(2,1)} %pad_maximum_fusion.kv_in, bf16[2,16,128,128]{3,2,1,0:T(8,128)(2,1)} %copy.73.q_in, bf16[2,16,128,128]{3,2,1,0:T(8,128)(2,1)} %bitcast.41, bf16[2,16,128,128]{3,2,1,0:T(8,128)(2,1)} %copy.74.do_in, ...), custom_call_target="tpu_custom_call" | custom-call | flops 46976204800 | bytes 31457280 | tf_op jit(solution)/shard_map/ring_backward/pallas_call | solution.py:217
  254.6 2.7 %copy.75 = bf16[16,32,2,4,128]{4,3,2,1,0:T(4,128)(2,1)} copy(bf16[16,32,2,4,128]{4,3,1,0,2:T(4,128)(2,1)} %bitcast.43) | data formatting | bytes 2097152 | tf_op jit(solution)/shard_map/transpose | solution.py:242
  257.4 0.1 fusion.1
  257.5 1.3 copy.78
  258.9 1.3 copy.77
  (24 shorter events, 0.6 us)
Async XLA Ops:
  0.6 5.3 %copy-start = (bf16[16,32,8,128]{3,2,1,0:T(8,128)(2,1)S(1)}, bf16[16,32,8,128]{3,2,1,0:T(8,128)(2,1)}, u32[]{:S(2)}) copy-start(bf16[16,32,8,128]{3,2,1,0:T(8,128)(2,1)} %param.9) | copy-start | bytes 3145732
  6.0 3.1 %copy-start.3 = (bf16[640,2,128]{2,1,0:T(2,128)(2,1)S(1)}, bf16[640,2,128]{2,1,0:T(2,128)(2,1)}, u32[]{:S(2)}) copy-start(bf16[640,2,128]{2,1,0:T(2,128)(2,1)} %param.12) | copy-start | bytes 983044
  6.0 3.1 %copy-start.4 = (bf16[640,2,128]{2,1,0:T(2,128)(2,1)S(1)}, bf16[640,2,128]{2,1,0:T(2,128)(2,1)}, u32[]{:S(2)}) copy-start(bf16[640,2,128]{2,1,0:T(2,128)(2,1)} %param.11) | copy-start | bytes 983044
  9.0 1.5 copy-start.2
  254.6 2.7 %copy-start.1 = (f32[2,2,320,256]{3,2,1,0:T(8,128)S(1)}, f32[2,2,320,256]{3,2,1,0:T(8,128)}, u32[]{:S(2)}) copy-start(f32[2,2,320,256]{3,2,1,0:T(8,128)} %get-tuple-element.6) | copy-start | bytes 3932164

commit v2 on v1

--- a/solution.py
+++ b/solution.py
@@ -12,10 +12,12 @@
 CORES = 2
 F32 = jnp.float32
 BF16 = jnp.bfloat16
-
-
-def ring_kernel(cp_size, sub_start, local_len, scale, kv_in, q_in, qt_in, do_in, dot_in, st_in, dq_out, dkv_out,
-                kvb, acc, rsb, qn, qt, don, dot, st, dqa, dqr, dqo,
+RUNS = 2
+EARLY_ITEMS = 88
+
+
+def ring_kernel(cp_size, sub_start, local_len, scale, early_items, kv_in, q_in, qt_in, do_in, dot_in, st_in, dq_out, dkv_out,
+                kvb, acc, rsb, qn, qt, don, dot, st, dqa, dqr, dqo, pbuf, dsbuf,
                 ag_send, ag_recv, rs_send, rs_recv, x_send, x_recv, loc_sem, out_sem):
     n_chip = cp_size // CORES
     n_hop = n_chip - 1
@@ -26,6 +28,7 @@
     sub_len = local_len * cp_size
     keys_local = 2 * key_tile
     own = 2 * n_hop
+    width = CORES * rows
 
     me = lax.axis_index('cp')
     chip, core = me // CORES, lax.rem(me, CORES)
@@ -59,7 +62,7 @@
 
     def part_of(ref, which):
         cut = pl.ds(which * rows, rows)
-        return ref.at[:, :, cut, :] if ref.shape[2] == CORES * rows and ref.shape[3] == head_dim else ref.at[:, :, :, cut]
+        return ref.at[:, :, cut, :] if ref is qn or ref is don else ref.at[:, :, :, cut]
 
     share = [remote(a, part_of(b, 1), x_send.at[i], x_recv.at[i], sibling) for i, (a, b) in enumerate(pairs)]
     local = [pltpu.make_async_copy(a, part_of(b, 0), loc_sem.at[i]) for i, (a, b) in enumerate(pairs)]
@@ -74,51 +77,97 @@
     def _(i):
         dqa[i // n_sub, lax.rem(i, n_sub)] = jnp.zeros(dqa.shape[2:], F32)
 
+    @pl.loop(0, acc.shape[0] * n_kv)
+    def _(i):
+        acc[i // n_kv, lax.rem(i, n_kv)] = jnp.zeros(acc.shape[2:], F32)
+
+    pbuf[...] = jnp.zeros(pbuf.shape, BF16)
+    dsbuf[...] = jnp.zeros(dsbuf.shape, BF16)
+
+    n_run = n_sub // RUNS
+    n_early = 2 + min(8, 2 * n_hop)
+    n_entry = n_early + 2 * n_hop
+
+    def place(e):
+        early = e < n_early
+        f = jnp.where(early, e - 2, e - n_early)
+        k = jnp.where(early, f // 2, n_hop - 1 - f // 2)
+        way = f % 2
+        mine = e < 2
+        slot = jnp.where(mine, own + e, way * n_hop + k)
+        half = jnp.where(mine, e, (k + way) % 2)
+        hop = k // 2 + 1
+        key_chip = jnp.where(mine, chip, lax.rem(chip + jnp.where(way == 1, hop, n_chip - hop), n_chip))
+        pos0 = (key_chip * CORES + core) * keys_local + half * key_tile
+        s_lo = jnp.minimum(jnp.maximum(pos0 - sub_start - span * chip - span + sub_len, 0) // sub_len, n_sub - 1)
+        return slot, pos0, s_lo // RUNS
+
+    counts, ends, taken = [], [], []
+    total = jnp.int32(0)
+    for e in range(n_entry):
+        n = n_kv * (n_run - place(jnp.int32(e))[2])
+        if e < n_early:
+            fits = jnp.int32(1) if e < 2 else (total + n <= early_items).astype(jnp.int32)
+            if len(taken) > 2:
+                fits = fits * taken[-1]
+            taken.append(fits)
+            n = n * fits
+        else:
+            f = e - n_early
+            i_early = 2 + 2 * (n_hop - 1 - f // 2) + f % 2
+            if i_early < n_early:
+                n = n * (1 - taken[i_early])
+        total = total + n
+        counts.append(n)
+        ends.append(total)
+
+    def item(i):
+        i = jnp.minimum(i, total - 1)
+        e, first = jnp.int32(0), jnp.int32(0)
+        for n, end in zip(counts, ends):
+            past = (i >= end).astype(jnp.int32)
+            e, first = e + past, first + past * n
+        slot, pos0, s_lo = place(e)
+        j, head = i - first, jnp.int32(0)
+        for m in range(1, n_kv):
+            head = head + (i - first >= m * (n_run - s_lo)).astype(jnp.int32)
+        return slot, head, (s_lo + j - head * (n_run - s_lo)) * RUNS, pos0
+
     for c in local:
         c.wait()
     for c in share:
         c.wait()
 
     exp_scale = scale * math.log2(math.e)
-    k_iota = lax.broadcasted_iota(jnp.int32, (key_tile, CORES * rows), 0).astype(F32)
-
-    def chunk(slot, key_chip, half, head):
-        pos0 = (key_chip * CORES + core) * keys_local + half * key_tile
-        t = pos0 - sub_start - span * chip - span + sub_len
-        s_lo = jnp.minimum(jnp.maximum(t, 0) // sub_len, n_sub)
+
+    def step(i, carry):
+        (slot_p, head_p, s_p), (slot, head, s, pos0) = carry
+        now = lax.rem(i, 2)
+        k, v = kvb[slot, head, :, :head_dim], kvb[slot, head, :, head_dim:]
+        s_t = [jnp.dot(k, qt[head, s + r], preferred_element_type=F32) for r in range(RUNS)]
+        dp_t = [jnp.dot(v, dot[head, s + r], preferred_element_type=F32) for r in range(RUNS)]
+        p_p, ds_p = pbuf[1 - now], dsbuf[1 - now]
+        q_p = qn[head_p, pl.ds(s_p, RUNS)].reshape(RUNS * width, head_dim)
+        do_p = don[head_p, pl.ds(s_p, RUNS)].reshape(RUNS * width, head_dim)
+        acc[slot_p, head_p, :, head_dim:] += jnp.dot(p_p, do_p, preferred_element_type=F32)
+        acc[slot_p, head_p, :, :head_dim] += jnp.dot(ds_p, q_p, preferred_element_type=F32)
+        k_t = kvb[slot_p, head_p, :, :head_dim].T
+        for r in range(RUNS):
+            dqa[head_p, s_p + r] += jnp.dot(k_t, ds_p[:, r * width:(r + 1) * width], preferred_element_type=F32)
         pos_f = pos0.astype(F32)
-        k = kvb[slot, head, :, :head_dim]
-        v = kvb[slot, head, :, head_dim:]
-        acc[slot, head] = jnp.zeros(acc.shape[2:], F32)
-
-        @pl.loop(s_lo, n_sub)
-        def _(s):
-            lse, delta = st[head, s, 0:1, :], st[head, s, 1:2, :]
-            lo, hi = st[head, s, 2:3, :] - pos_f, st[head, s, 3:4, :] - pos_f
-            s_t = jnp.dot(k, qt[head, s], preferred_element_type=F32)
-            dp_t = jnp.dot(v, dot[head, s], preferred_element_type=F32)
+        k_iota = lax.broadcasted_iota(jnp.int32, (key_tile, width), 0).astype(F32)
+        for r in range(RUNS):
+            lse, delta = st[head, s + r, 0:1, :], st[head, s + r, 1:2, :]
+            lo, hi = st[head, s + r, 2:3, :] - pos_f, st[head, s + r, 3:4, :] - pos_f
             ok = (k_iota >= lo) & (k_iota <= hi)
-            p = jnp.where(ok, jnp.exp2(s_t * exp_scale - lse), 0.0)
-            ds = (p * (dp_t - delta)).astype(BF16)
-            acc[slot, head, :, head_dim:] += jnp.dot(p.astype(BF16), don[head, s], preferred_element_type=F32)
-            acc[slot, head, :, :head_dim] += jnp.dot(ds, qn[head, s], preferred_element_type=F32)
-            dqa[head, s] += lax.dot_general(ds, k, (((0,), (0,)), ((), ())), preferred_element_type=F32)
-
-    def unit(way, k):
-        if way is None:
-            slot, key_chip, half = own + k, chip, k
-        else:
-            hop = k // 2 + 1
-            slot, half = way * n_hop + k, half_of(way, k)
-            key_chip = lax.rem(chip + (hop if way else n_chip - hop), n_chip)
-        for head in range(n_kv):
-            chunk(slot, key_chip, half, head)
-
-    def event(k):
-        for way in range(2):
-            gather(way, k).wait_recv()
-            if k + 2 < n_hop:
-                gather(way, k + 2).start()
+            p = jnp.where(ok, jnp.exp2(s_t[r] * exp_scale - lse), 0.0)
+            pbuf[now, :, r * width:(r + 1) * width] = p.astype(BF16)
+            dsbuf[now, :, r * width:(r + 1) * width] = (p * (dp_t[r] - delta)).astype(BF16)
+        return (slot, head, s), item(i + 1)
+
+    def advance(state, target):
+        i, carry = state
+        return jnp.maximum(i, target), lax.fori_loop(i, target, step, carry)
 
     def add(dst, src):
         steps = n_kv * 4
@@ -129,22 +178,41 @@
             h, r = i // 4, pl.ds(pl.multiple_of(lax.rem(i, 4) * cut, 8), cut)
             acc[dst, h, r, :] += rsb[src, h, r, :]
 
-    units = [(None, 0), (None, 1)] + [(way, k) for k in range(n_hop) for way in range(2)]
-    done = units[:n_hop]
-    for k in range(n_hop):
-        unit(*done[k])
-        event(k)
-    for k in reversed(range(n_hop)):
+    def end_of(e):
+        out = jnp.int32(0)
+        for v, n in enumerate(counts):
+            out = out + jnp.where(e >= v, n, 0)
+        return out
+
+    def gather_event(k, state):
+        share_items = (early_items * (k + 1)) // (n_hop + 1)
+        state = advance(state, jnp.minimum(share_items, end_of(jnp.minimum(2 * k + 1, n_early - 1))))
         for way in range(2):
-            if (way, k) not in done:
-                unit(way, k)
-            if k + 2 < n_hop:
-                reduce_copy(way, k + 2).wait_recv()
-                add(way * n_hop + k, way * n_hop + k + 2)
-            reduce_copy(way, k).start()
-    for u in ((None, 0), (None, 1)):
-        if u not in done:
-            unit(*u)
+            i = way * n_hop + k
+            remote(kvb.at[i], kvb.at[i], ag_send.at[i], ag_recv.at[i], nbr[way]).wait_recv()
+
+            @pl.when(k + 2 < n_hop)
+            def _():
+                remote(kvb.at[i], kvb.at[i + 2], ag_send.at[i + 2], ag_recv.at[i + 2], nbr[way]).start()
+        return state
+
+    def reduce_event(m, state):
+        k, way = n_hop - 1 - m // 2, m % 2
+        i = way * n_hop + k
+        peer = jnp.where(way == 0, left, right)
+        state = advance(state, end_of(n_early + m) + 1)
+
+        @pl.when(k + 2 < n_hop)
+        def _():
+            remote(acc.at[i + 2], rsb.at[i + 2], rs_send.at[i + 2], rs_recv.at[i + 2], peer).wait_recv()
+            add(i, i + 2)
+
+        remote(acc.at[i], rsb.at[i], rs_send.at[i], rs_recv.at[i], peer).start()
+        return state
+
+    state = (jnp.int32(0), (item(jnp.int32(0))[:3], item(jnp.int32(0))))
+    state = lax.fori_loop(0, n_hop, gather_event, state)
+    state = lax.fori_loop(0, 2 * n_hop, reduce_event, state)
     swap = remote(part_of(dqa, 1), dqr, x_send.at[len(pairs)], x_recv.at[len(pairs)], sibling)
     swap.start()
     swap.wait_recv()
@@ -152,7 +220,7 @@
     @pl.loop(0, n_kv * n_sub)
     def _(i):
         h, s = i // n_sub, lax.rem(i, n_sub)
-        dqo[h, s] = ((dqa[h, s, :rows, :] + dqr[h, s]) * scale).astype(BF16)
+        dqo[h, s] = ((dqa[h, s, :, :rows] + dqr[h, s]) * scale).astype(BF16).T
 
     put_dq = pltpu.make_async_copy(dqo, dq_out, out_sem.at[0])
     put_dq.start()
@@ -215,7 +283,7 @@
         hbm = pl.BlockSpec(memory_space=pl.ANY)
         dma = pltpu.SemaphoreType.DMA
         dq, dkv = pl.pallas_call(
-            functools.partial(ring_kernel, cp_size, sub_start, local_len, scale),
+            functools.partial(ring_kernel, cp_size, sub_start, local_len, scale, EARLY_ITEMS),
             name='ring_backward',
             out_shape=(jax.ShapeDtypeStruct((n_kv, n_sub, rows, head_dim), BF16),
                        jax.ShapeDtypeStruct((2, n_kv, half, 2 * head_dim), F32)),
@@ -230,9 +298,11 @@
                 pltpu.VMEM((n_kv, n_sub, CORES * rows, head_dim), BF16),
                 pltpu.VMEM((n_kv, n_sub, head_dim, CORES * rows), BF16),
                 pltpu.VMEM((n_kv, n_sub, 8, CORES * rows), F32),
-                pltpu.VMEM((n_kv, n_sub, CORES * rows, head_dim), F32),
-                pltpu.VMEM((n_kv, n_sub, rows, head_dim), F32),
+                pltpu.VMEM((n_kv, n_sub, head_dim, CORES * rows), F32),
+                pltpu.VMEM((n_kv, n_sub, head_dim, rows), F32),
                 pltpu.VMEM((n_kv, n_sub, rows, head_dim), BF16),
+                pltpu.VMEM((2, half, RUNS * CORES * rows), BF16),
+                pltpu.VMEM((2, half, RUNS * CORES * rows), BF16),
                 dma((2 * n_hop,)), dma((2 * n_hop,)), dma((2 * n_hop,)), dma((2 * n_hop,)),
                 dma((6,)), dma((6,)), dma((6,)), dma((2,)),
             ],

time: 261 us -> 219 us (0.84)
  Pallas kernels: 236 us -> 194 us
    pallas_call x1, Pallas kernels: 236 us -> 194 us  [local_backward(): pl.pallas_call(functools.partial(ring_kernel, cp_size, sub_start, local_l...]
where the time goes in v2:
time: 219 us; the launch traced here: 218 us
  Pallas kernels  194 us (89%)
  local copies, waits for them, and re-layouts  16.3 us (7%)
  other arithmetic  6.72 us (3%)
    pallas_call x1, Pallas kernels, local_backward(): pl.pallas_call(functools.partial(ring_kernel, cp_size, sub_start, local_l...  194 us
    reshape x4, local copies, waits for them, and re-layouts, by_head(): return x.reshape((n_kv, n_sub, rows) + x.shape[4:])  5.89 us

profile of v2, /device:TPU:22, one launch (start us, length us, event | category | flops | bytes accessed | tf_op | source)
XLA Modules:
  0.0 217.9 jit_solution(15640823858663150743)
XLA Ops:
  0.7 0.8 slice.19
  1.6 3.0 %convert_reduce_fusion = f32[16,32]{1,0:T(8,128)S(1)} fusion(s32[16,32]{1,0:T(8,128)S(1)} %constant_dynamic-slice_fusion, s32[10240]{0:T(1024)} %param.13), kind=kLoop, calls=%fused_computation | loop fusion | flops 15728128 | bytes 45056 | tf_op jit(solution)/shard_map/reduce_sum | solution.py:274
  4.9 0.8 broadcast_multiply_fusion
  5.8 0.1 copy.66
  6.0 1.9 fusion
  7.9 0.1 copy.83
  8.0 0.1 copy.67
  8.2 0.8 stack.8.st_in
  9.0 0.1 copy_bitcast_fusion
  9.1 0.9 pad_maximum_fusion.kv_in
  10.0 0.5 copy-done.2
  10.5 0.2 copy.60
  10.7 0.7 copy.61
  11.4 1.2 copy.73.q_in
  12.7 1.7 copy.62
  14.4 0.2 copy.63
  14.6 0.7 copy.64
  15.3 1.2 copy.74.do_in
  16.6 1.7 copy.65
  18.3 194.1 %ring_backward.1 = (bf16[2,16,128,128]{3,2,1,0:T(8,128)(2,1)}, f32[2,2,320,256]{3,2,1,0:T(8,128)}) custom-call(bf16[2,2,320,256]{3,2,1,0:T(8,128)(2,1)} %pad_maximum_fusion.kv_in, bf16[2,16,128,128]{3,2,1,0:T(8,128)(2,1)} %copy.73.q_in, bf16[2,16,128,128]{3,2,1,0:T(8,128)(2,1)} %bitcast.41, bf16[2,16,128,128]{3,2,1,0:T(8,128)(2,1)} %copy.74.do_in, ...), custom_call_target="tpu_custom_call" | custom-call | flops 46976204800 | bytes 31457280 | tf_op jit(solution)/shard_map/ring_backward/pallas_call | solution.py:285
  212.4 2.7 %copy.75 = bf16[16,32,2,4,128]{4,3,2,1,0:T(4,128)(2,1)} copy(bf16[16,32,2,4,128]{4,3,1,0,2:T(4,128)(2,1)} %bitcast.43) | data formatting | bytes 2097152 | tf_op jit(solution)/shard_map/transpose | solution.py:312
  215.1 0.1 fusion.1
  215.2 1.3 copy.78
  216.6 1.3 copy.77
  (24 shorter events, 0.6 us)
Async XLA Ops:
  0.6 5.3 %copy-start = (bf16[16,32,8,128]{3,2,1,0:T(8,128)(2,1)S(1)}, bf16[16,32,8,128]{3,2,1,0:T(8,128)(2,1)}, u32[]{:S(2)}) copy-start(bf16[16,32,8,128]{3,2,1,0:T(8,128)(2,1)} %param.9) | copy-start | bytes 3145732
  6.0 3.1 %copy-start.3 = (bf16[640,2,128]{2,1,0:T(2,128)(2,1)S(1)}, bf16[640,2,128]{2,1,0:T(2,128)(2,1)}, u32[]{:S(2)}) copy-start(bf16[640,2,128]{2,1,0:T(2,128)(2,1)} %param.12) | copy-start | bytes 983044
  6.0 3.1 %copy-start.4 = (bf16[640,2,128]{2,1,0:T(2,128)(2,1)S(1)}, bf16[640,2,128]{2,1,0:T(2,128)(2,1)}, u32[]{:S(2)}) copy-start(bf16[640,2,128]{2,1,0:T(2,128)(2,1)} %param.11) | copy-start | bytes 983044
  9.0 1.5 copy-start.2
  212.3 2.7 %copy-start.1 = (f32[2,2,320,256]{3,2,1,0:T(8,128)S(1)}, f32[2,2,320,256]{3,2,1,0:T(8,128)}, u32[]{:S(2)}) copy-start(f32[2,2,320,256]{3,2,1,0:T(8,128)} %get-tuple-element.6) | copy-start | bytes 3932164

commit v3 on v2

v3 whole, which is shorter than its diff:
```python
import functools
import math

import jax
import jax.numpy as jnp
from jax import lax
from jax.experimental import pallas as pl
from jax.experimental.pallas import tpu as pltpu
from jax.sharding import PartitionSpec as P

MESH = pl.DeviceIdType.MESH
CORES = 2
LANES = 128
RUNS = 2
UNROLL = 2
EARLY_ITEMS = 98
F32 = jnp.float32
BF16 = jnp.bfloat16


def ring_kernel(cp_size, sub_start, scale, kv_in, q_in, o_in, do_in, lse_in, doc_in, dq_out, dkv_out,
                kvb, acc, rsb, raw_q, raw_do, raw_o, lse, docs, qn, qt, don, dot, lines, key_doc, dqa, dqr, dqo, pbuf, dsbuf,
                ag_send, ag_recv, rs_send, rs_recv, x_send, x_recv, loc_sem, out_sem):
    n_chip = cp_size // CORES
    n_hop = n_chip - 1
    n_sub, local_len, n_kv, group, head_dim = q_in.shape
    rows = local_len * group
    width = CORES * rows
    key_tile = kv_in.shape[2]
    span = local_len * CORES
    sub_len = local_len * cp_size
    keys_local = 2 * key_tile
    own = 2 * n_hop

    me = lax.axis_index('cp')
    chip, core = me // CORES, lax.rem(me, CORES)
    right = lax.rem(me + CORES, cp_size)
    left = lax.rem(me + cp_size - CORES, cp_size)
    sibling = me + 1 - 2 * core
    nbr = (right, left)

    barrier = pltpu.get_barrier_semaphore()
    for peer in (right, left, sibling):
        pl.semaphore_signal(barrier, inc=1, device_id={'cp': peer}, device_id_type=MESH)
    pl.semaphore_wait(barrier, 3)

    def remote(src, dst, send, recv, peer):
        return pltpu.make_async_remote_copy(src_ref=src, dst_ref=dst, send_sem=send, recv_sem=recv,
                                            device_id={'cp': peer}, device_id_type=MESH)

    for j in range(2):
        for way in range(2):
            i = way * n_hop + j
            remote(kv_in.at[(j + way) % 2], kvb.at[i], ag_send.at[i], ag_recv.at[i], nbr[way]).start()
    share = [remote(q_in, raw_q.at[1], x_send.at[0], x_recv.at[0], sibling),
             remote(do_in, raw_do.at[1], x_send.at[1], x_recv.at[1], sibling)]
    local = [pltpu.make_async_copy(a, b, loc_sem.at[i]) for i, (a, b) in enumerate((
        (doc_in, docs), (lse_in, lse), (do_in, raw_do.at[0]), (o_in, raw_o), (q_in, raw_q.at[0]), (kv_in, kvb.at[pl.ds(own, 2)])))]
    for c in local + share:
        c.start()

    def mine(which):
        return lines.at[:, :, :, pl.ds(which * rows, rows)]

    share_lines = remote(mine(0), mine(1), x_send.at[2], x_recv.at[2], sibling)

    @pl.loop(0, n_sub)
    def _(s):
        for h in range(n_kv):
            dqa[h, s] = jnp.zeros(dqa.shape[2:], F32)

    @pl.loop(0, acc.shape[0])
    def _(i):
        for h in range(n_kv):
            acc[i, h] = jnp.zeros(acc.shape[2:], F32)

    pbuf[...] = jnp.zeros(pbuf.shape, BF16)
    dsbuf[...] = jnp.zeros(dsbuf.shape, BF16)
    local[0].wait()
    tiles = keys_local // LANES

    @pl.loop(0, n_chip * tiles)
    def _(i):
        b, r = i // tiles, lax.rem(i, tiles)
        row = (b * CORES + core) * tiles + r
        key_doc[b, pl.ds(pl.multiple_of(r * LANES, LANES), LANES), :] = jnp.broadcast_to(docs[pl.ds(row, 1), :], (LANES, LANES)).T

    lane = lax.broadcasted_iota(jnp.int32, (8, rows), 1)
    sub = lax.broadcasted_iota(jnp.int32, (8, rows), 0)
    for c in local[1:4]:
        c.wait()

    @pl.loop(0, n_sub)
    def _(s):
        rep = jnp.concatenate([lse[s]] * (LANES // local_len), axis=1)
        wide = jnp.take_along_axis(rep, lane // group, axis=1)
        for h in range(n_kv):
            line = jnp.sum(jnp.where(sub - group * h == lane % group, wide, 0.0), axis=0, keepdims=True) * math.log2(math.e)
            prod = raw_do[0, s, :, h].reshape(rows, head_dim).astype(F32) * raw_o[s, :, h].reshape(rows, head_dim).astype(F32)
            total = jnp.broadcast_to(jnp.sum(prod, axis=1, keepdims=True), (rows, LANES)).T
            first = sub_start + s * sub_len + me * local_len
            doc_row = jnp.broadcast_to(docs[pl.ds(first // LANES, 1), :], (8, LANES))
            doc = jnp.take_along_axis(doc_row, lax.rem(first, LANES) + lane // group, axis=1).astype(F32)
            lines[h, s, :, :rows] = jnp.where(sub == 0, line, jnp.where(sub == 1, total[:8, :], doc))

    share_lines.start()

    def spread(c):
        @pl.loop(0, n_sub)
        def _(s):
            for h in range(n_kv):
                for raw, nat, tr in ((raw_q, qn, qt), (raw_do, don, dot)):
                    x = raw[c, s, :, h].reshape(rows, head_dim)
                    nat[h, s, c * rows:(c + 1) * rows, :] = x
                    tr[h, s, :, c * rows:(c + 1) * rows] = x.T

    for c in local[4:]:
        c.wait()
    spread(0)
    for c in share:
        c.wait()
    spread(1)
    share_lines.wait()

    n_run = n_sub // RUNS
    n_early = 2 + min(8, 2 * n_hop)
    n_late = 2 * n_hop * n_kv

    def place(e):
        early = e < n_early
        f = jnp.where(early, e - 2, e - n_early)
        k = jnp.where(early, f // 2, n_hop - 1 - f // (2 * n_kv))
        way = f % 2
        mine = e < 2
        slot = jnp.where(mine, own + e, way * n_hop + k)
        half = jnp.where(mine, e, (k + way) % 2)
        hop = k // 2 + 1
        key_chip = jnp.where(mine, chip, lax.rem(chip + jnp.where(way == 1, hop, n_chip - hop), n_chip))
        pos0 = (key_chip * CORES + core) * keys_local + half * key_tile
        s_lo = jnp.minimum(jnp.maximum(pos0 - sub_start - span * chip - span + sub_len, 0) // sub_len, n_sub - 1)
        return slot, key_chip, half, s_lo // RUNS

    counts, ends, taken = [], [], []
    total = jnp.int32(0)
    for e in range(n_early + n_late):
        n = n_run - place(jnp.int32(e))[3]
        if e < n_early:
            n = n * n_kv
            fits = jnp.int32(1) if e < 2 else (total + n <= EARLY_ITEMS).astype(jnp.int32)
            if e > 2:
                fits = fits * taken[-1]
            taken.append(fits)
            n = n * fits
        else:
            f = e - n_early
            i_early = 2 + 2 * (n_hop - 1 - f // (2 * n_kv)) + f % 2
            if i_early < n_early:
                n = n * (1 - taken[i_early])
        total = total + n
        counts.append(n)
        ends.append(total)

    n_taken = taken[0]
    for t in taken[1:]:
        n_taken = n_taken + t

    def following(at):
        i, e, j, n = at
        over = j + 1 >= n
        e1 = e + 1
        e1 = jnp.where(e1 == n_taken, n_early, e1)
        f = e1 - n_early
        again = (f >= 0) & (2 + 2 * (n_hop - 1 - f // (2 * n_kv)) + f % 2 < n_taken)
        e1 = jnp.minimum(jnp.where(again, e1 + 1, e1), n_early + n_late - 1)
        e, j = jnp.where(over, e1, e), jnp.where(over, 0, j + 1)
        slot, key_chip, half, s_lo = place(e)
        nth = jnp.int32(0)
        for m in range(1, n_kv):
            nth = nth + (j >= m * (n_run - s_lo)).astype(jnp.int32)
        head = jnp.where(e < n_early, nth, (e - n_early) // 2 % n_kv)
        n = (n_run - s_lo) * jnp.where(e < n_early, n_kv, 1)
        i = i + 1
        s = (s_lo + j - jnp.where(e < n_early, nth, 0) * (n_run - s_lo)) * RUNS
        return (slot, head, s, key_chip, half, (i < total).astype(jnp.int32)), (i, e, j, n)

    exp_scale = scale * math.log2(math.e)
    k_iota = lax.broadcasted_iota(jnp.int32, (key_tile, width), 0)
    col = lax.broadcasted_iota(jnp.int32, (1, width), 1)
    q_off = sub_start + jnp.where(col < rows, me, sibling) * local_len + lax.rem(col, rows) // group

    def one(now, carry):
        (slot_p, head_p, s_p), (slot, head, s, key_chip, half, live), at = carry
        then, at = following(at)
        k, v = kvb[slot, head, :, :head_dim], kvb[slot, head, :, head_dim:]
        s_t = [jnp.dot(k, qt[head, s + r], preferred_element_type=F32) for r in range(RUNS)]
        dp_t = [jnp.dot(v, dot[head, s + r], preferred_element_type=F32) for r in range(RUNS)]
        p_p, ds_p = pbuf[1 - now], dsbuf[1 - now]
        q_p = qn[head_p, pl.ds(s_p, RUNS)].reshape(RUNS * width, head_dim)
        do_p = don[head_p, pl.ds(s_p, RUNS)].reshape(RUNS * width, head_dim)
        acc[slot_p, head_p, :, head_dim:] += jnp.dot(p_p, do_p, preferred_element_type=F32)
        acc[slot_p, head_p, :, :head_dim] += jnp.dot(ds_p, q_p, preferred_element_type=F32)
        k_t = kvb[slot_p, head_p, :, :head_dim].T
        for r in range(RUNS):
            dqa[head_p, s_p + r] += jnp.dot(k_t, ds_p[:, r * width:(r + 1) * width], preferred_element_type=F32)
        docs_k = key_doc[key_chip, pl.ds(pl.multiple_of(half * key_tile, 8), key_tile), :]
        docs_k = jnp.concatenate([docs_k] * (width // LANES), axis=1)
        pos0 = (key_chip * CORES + core) * keys_local + half * key_tile
        for r in range(RUNS):
            lse_r, delta_r, doc_r = [lines[head, s + r, m:m + 1, :] for m in range(3)]
            last = jnp.where(live == 1, q_off + (s + r) * sub_len - pos0, -1)
            ok = (docs_k == doc_r.astype(jnp.int32)) & (k_iota <= last)
            p = jnp.where(ok, jnp.exp2(s_t[r] * exp_scale - lse_r), 0.0)
            pbuf[now, :, r * width:(r + 1) * width] = p.astype(BF16)
            dsbuf[now, :, r * width:(r + 1) * width] = (p * (dp_t[r] - delta_r)).astype(BF16)
        return (slot, head, s), then, at

    def advance(state, target):
        i, carry = state
        m = jnp.maximum(target - i, 0) // UNROLL

        def step(_, carry):
            for u in range(UNROLL):
                carry = one(u % 2, carry)
            return carry

        return i + m * UNROLL, lax.fori_loop(0, m, step, carry)

    def end_of(e):
        out = jnp.int32(0)
        for v, n in enumerate(counts):
            out = out + jnp.where(e >= v, n, 0)
        return out

    def gather_event(k, state):
        goal = (EARLY_ITEMS * (k + 1)) // n_hop
        state = advance(state, jnp.minimum(goal, end_of(jnp.minimum(2 * k + 1, n_early - 1))))
        for way in range(2):
            i = way * n_hop + k
            remote(kvb.at[i], kvb.at[i], ag_send.at[i], ag_recv.at[i], nbr[way]).wait_recv()

            @pl.when(k + 2 < n_hop)
            def _():
                remote(kvb.at[i], kvb.at[i + 2], ag_send.at[i + 2], ag_recv.at[i + 2], nbr[way]).start()
        return state

    def add(dst, src, head):
        cut = key_tile // 4

        @pl.loop(0, 4)
        def _(i):
            r = pl.ds(pl.multiple_of(i * cut, 8), cut)
            acc[dst, head, r, :] += rsb[src, head, r, :]

    def partial(i, head, peer):
        return remote(acc.at[i, head], rsb.at[i, head], rs_send.at[i, head], rs_recv.at[i, head], peer)

    def reduce_event(m, state):
        k, head, way = n_hop - 1 - m // (2 * n_kv), m // 2 % n_kv, m % 2
        i = way * n_hop + k
        peer = jnp.where(way == 0, left, right)
        state = advance(state, end_of(n_early + m) + UNROLL)

        @pl.when(k + 2 < n_hop)
        def _():
            partial(i + 2, head, peer).wait_recv()
            add(i, i + 2, head)

        partial(i, head, peer).start()
        return state

    zero = jnp.int32(0)
    start, at = following((zero - 1, zero, zero - 1, zero + 1))
    state = (zero, (start[:3], start, at))
    state = lax.fori_loop(0, n_hop, gather_event, state)
    state = lax.fori_loop(0, n_late, reduce_event, state)
    half_rows = lambda which: dqa.at[:, :, :, pl.ds(which * rows, rows)]
    swap = remote(half_rows(1), dqr, x_send.at[3], x_recv.at[3], sibling)
    swap.start()
    swap.wait_recv()

    @pl.loop(0, n_sub)
    def _(s):
        for h in range(n_kv):
            x = ((dqa[h, s, :, :rows] + dqr[h, s]) * scale).astype(BF16).T
            dqo[s, :, h] = x.reshape(local_len, group, head_dim)

    put_dq = pltpu.make_async_copy(dqo, dq_out, out_sem.at[0])
    put_dq.start()
    for head in range(n_kv):
        for k in reversed(range(2)):
            for way in range(2):
                partial(way * n_hop + k, head, nbr[1 - way]).wait_recv()
                add(own + (k + way) % 2, way * n_hop + k, head)

    @pl.loop(0, 2)
    def _(half):
        for h in range(n_kv):
            acc[own + half, h, :, :head_dim] = acc[own + half, h, :, :head_dim] * scale

    put_kv = pltpu.make_async_copy(acc.at[pl.ds(own, 2)], dkv_out, out_sem.at[1])
    put_kv.start()
    swap.wait_send()
    for way in range(2):
        for j in range(n_hop):
            i = way * n_hop + j
            remote(kvb.at[i], kvb.at[i], ag_send.at[i], ag_recv.at[i], nbr[way]).wait_send()
            for head in range(n_kv):
                partial(i, head, nbr[1 - way]).wait_send()
    put_dq.wait()
    put_kv.wait()


def solution(mesh):
    cp_size = mesh.shape['cp']
    q_spec = P(None, 'cp', 'tp', None)
    lse_spec = P(None, 'cp', 'tp')
    kv_spec = P('cp', 'tp', None)

    def local_backward(query, out_act, out_grad, row_lse, key_act, value_act, doc_ids):
        n_sub, local_len, n_heads, head_dim = query.shape
        keys_local, n_kv = key_act.shape[0], key_act.shape[1]
        group = n_heads // n_kv
        sub_start = keys_local * cp_size - n_sub * local_len * cp_size
        rows = local_len * group
        half = keys_local // 2
        n_chip = cp_size // CORES
        n_hop = n_chip - 1
        n_slot = 2 * n_hop + 2
        q5 = (n_sub, local_len, n_kv, group, head_dim)
        cut = lambda x: jnp.transpose(x.reshape(2, half, n_kv, head_dim), (0, 2, 1, 3))
        kv = jnp.concatenate([cut(key_act), cut(value_act)], axis=-1)
        flops = 2 * 5 * n_kv * n_sub * 2 * rows * head_dim * keys_local * n_hop
        hbm = pl.BlockSpec(memory_space=pl.ANY)
        dma = pltpu.SemaphoreType.DMA
        vmem = pltpu.VMEM
        dq, dkv = pl.pallas_call(
            functools.partial(ring_kernel, cp_size, sub_start, head_dim ** -0.5),
            name='ring_backward',
            out_shape=(jax.ShapeDtypeStruct(q5, BF16), jax.ShapeDtypeStruct((2, n_kv, half, 2 * head_dim), F32)),
            in_specs=[hbm] * 6,
            out_specs=(hbm, hbm),
            scratch_shapes=[
                vmem((n_slot, n_kv, half, 2 * head_dim), BF16),
                vmem((n_slot, n_kv, half, 2 * head_dim), F32),
                vmem((2 * n_hop, n_kv, half, 2 * head_dim), F32),
                vmem((CORES,) + q5, BF16),
                vmem((CORES,) + q5, BF16),
                vmem(q5, BF16),
                vmem((n_sub, n_heads, local_len), F32),
                vmem((doc_ids.shape[0] // LANES, LANES), jnp.int32),
                vmem((n_kv, n_sub, CORES * rows, head_dim), BF16),
                vmem((n_kv, n_sub, head_dim, CORES * rows), BF16),
                vmem((n_kv, n_sub, CORES * rows, head_dim), BF16),
                vmem((n_kv, n_sub, head_dim, CORES * rows), BF16),
                vmem((n_kv, n_sub, 8, CORES * rows), F32),
                vmem((n_chip, keys_local, LANES), jnp.int32),
                vmem((n_kv, n_sub, head_dim, CORES * rows), F32),
                vmem((n_kv, n_sub, head_dim, rows), F32),
                vmem(q5, BF16),
                vmem((2, half, RUNS * CORES * rows), BF16),
                vmem((2, half, RUNS * CORES * rows), BF16),
                dma((2 * n_hop,)), dma((2 * n_hop,)), dma((2 * n_hop, n_kv)), dma((2 * n_hop, n_kv)),
                dma((4,)), dma((4,)), dma((6,)), dma((2,)),
            ],
            compiler_params=pltpu.CompilerParams(collective_id=0, has_side_effects=True, vmem_limit_bytes=62 * 1024 * 1024),
            cost_estimate=pl.CostEstimate(flops=flops, bytes_accessed=30 * 2 ** 20, transcendentals=0),
        )(kv, query.reshape(q5), out_act.reshape(q5), out_grad.reshape(q5), jnp.swapaxes(row_lse, 1, 2), doc_ids.reshape(-1, LANES))
        dkv = jnp.transpose(dkv, (0, 2, 1, 3)).reshape(keys_local, n_kv, 2 * head_dim)
        return dq.reshape(query.shape), dkv[..., :head_dim], dkv[..., head_dim:]

    return jax.shard_map(local_backward, mesh=mesh, in_specs=(q_spec, q_spec, q_spec, lse_spec, kv_spec, kv_spec, P()),
                         out_specs=(q_spec, kv_spec, kv_spec), check_vma=False)
```

time: 219 us -> 188 us (0.86)
  Pallas kernels: 194 us -> 180 us
  local copies, waits for them, and re-layouts: 16.3 us -> 6.31 us
  other arithmetic: 6.72 us -> 0.91 us
    pallas_call x1, Pallas kernels: 194 us -> 180 us  [local_backward(): pl.pallas_call(functools.partial(ring_kernel, cp_size, sub_start, head_di...]
    reshape x4 -> x0, local copies, waits for them, and re-layouts: 5.89 us -> none  [by_head(): return x.reshape((n_kv, n_sub, rows) + x.shape[4:])]
    transpose x4 -> x0, local copies, waits for them, and re-layouts: 4.17 us -> none  [the longest x1 2.69 us: local_backward(): jnp.moveaxis(dq.reshape(n_kv, n_sub, local_len, group, head_dim), 0, 2)]
    reduce_sum x1 -> x0, other arithmetic: 3.03 us -> none  [local_backward(): jnp.sum((doc_ids[None, None, :] < q_doc[:, :, None]).astype(F32), axis=-1)]
where the time goes in v3:
time: 188 us
  Pallas kernels  180 us (96%)
  local copies, waits for them, and re-layouts  6.31 us (3%)
    pallas_call x1, Pallas kernels, local_backward(): pl.pallas_call(functools.partial(ring_kernel, cp_size, sub_start, head_di...  180 us

profile of v3, /device:TPU:22, one launch (start us, length us, event | category | flops | bytes accessed | tf_op | source)
XLA Modules:
  0.0 187.5 jit_solution(3687897879289350461)
XLA Ops:
  0.6 1.2 copy_bitcast_fusion
  1.8 0.9 pad_maximum_fusion.kv_in
  2.7 179.6 %ring_backward.1 = (bf16[16,32,2,4,128]{4,3,2,1,0:T(4,128)(2,1)}, f32[2,2,320,256]{3,2,1,0:T(8,128)}) custom-call(bf16[2,2,320,256]{3,2,1,0:T(8,128)(2,1)} %pad_maximum_fusion.kv_in, bf16[16,32,2,4,128]{4,3,2,1,0:T(4,128)(2,1)} %bitcast.19, bf16[16,32,2,4,128]{4,3,2,1,0:T(4,128)(2,1)} %bitcast.20, bf16[16,32,2,4,128]{4,3,2,1,0:T(4,128)(2,1)} %bitcast.21, ...), custom_call_target="tpu_custom_call" | custom-call | flops 46976204800 | bytes 31457280 | tf_op jit(solution)/shard_map/ring_backward/pallas_call | solution.py:336
  182.4 1.4 copy.14
  183.8 0.1 fusion
  183.9 0.0 copy-start
  183.9 1.3 copy.16
  185.2 1.3 copy.15
  186.6 0.0 copy-done
  186.6 1.0 copy.24
Async XLA Ops:
  183.9 2.7 %copy-start = (bf16[16,32,2,4,128]{4,3,2,1,0:T(4,128)(2,1)S(1)}, bf16[16,32,2,4,128]{4,3,2,1,0:T(4,128)(2,1)}, u32[]{:S(2)}) copy-start(bf16[16,32,2,4,128]{4,3,2,1,0:T(4,128)(2,1)} %get-tuple-element.5) | copy-start | bytes 3145732

commit v4 on v3

--- a/solution.py
+++ b/solution.py
@@ -13,13 +13,13 @@
 LANES = 128
 RUNS = 2
 UNROLL = 2
-EARLY_ITEMS = 98
+EARLY_ITEMS = (36, 40)
 F32 = jnp.float32
 BF16 = jnp.bfloat16
 
 
-def ring_kernel(cp_size, sub_start, scale, kv_in, q_in, o_in, do_in, lse_in, doc_in, dq_out, dkv_out,
-                kvb, acc, rsb, raw_q, raw_do, raw_o, lse, docs, qn, qt, don, dot, lines, key_doc, dqa, dqr, dqo, pbuf, dsbuf,
+def ring_kernel(cp_size, sub_start, scale, kv_in, q_in, o_in, do_in, lse_in, doc_in, dq_out, dk_out, dv_out,
+                kvb, acc, rsb, raw_q, raw_do, raw_o, lse, docs, qn, qt, don, dot, lines, key_doc, dqa, dqr, dqo, dko, dvo, pbuf, dsbuf,
                 ag_send, ag_recv, rs_send, rs_recv, x_send, x_recv, loc_sem, out_sem):
     n_chip = cp_size // CORES
     n_hop = n_chip - 1
@@ -48,10 +48,25 @@
         return pltpu.make_async_remote_copy(src_ref=src, dst_ref=dst, send_sem=send, recv_sem=recv,
                                             device_id={'cp': peer}, device_id_type=MESH)
 
-    for j in range(2):
+    def gather(way, k, head, src=None):
+        i = way * n_hop + k
+        return remote(kvb.at[i, head] if src is None else src, kvb.at[i, head], ag_send.at[i, head], ag_recv.at[i, head], nbr[way])
+
+    def gather_own(head):
+        for j in range(2):
+            for way in range(2):
+                gather(way, j, head, kv_in.at[(j + way) % 2, head]).start()
+
+    def pass_on(k, head):
         for way in range(2):
-            i = way * n_hop + j
-            remote(kv_in.at[(j + way) % 2], kvb.at[i], ag_send.at[i], ag_recv.at[i], nbr[way]).start()
+            gather(way, k, head).wait_recv()
+            i = way * n_hop + k
+
+            @pl.when(k + 2 < n_hop)
+            def _():
+                gather(way, k + 2, head, kvb.at[i, head]).start()
+
+    gather_own(0)
     share = [remote(q_in, raw_q.at[1], x_send.at[0], x_recv.at[0], sibling),
              remote(do_in, raw_do.at[1], x_send.at[1], x_recv.at[1], sibling)]
     local = [pltpu.make_async_copy(a, b, loc_sem.at[i]) for i, (a, b) in enumerate((
@@ -117,6 +132,7 @@
     for c in local[4:]:
         c.wait()
     spread(0)
+    pass_on(0, 0)
     for c in share:
         c.wait()
     spread(1)
@@ -124,12 +140,13 @@
 
     n_run = n_sub // RUNS
     n_early = 2 + min(8, 2 * n_hop)
-    n_late = 2 * n_hop * n_kv
+    n_block = n_early + 2 * n_hop
 
     def place(e):
+        head, e = e // n_block, lax.rem(e, n_block)
         early = e < n_early
         f = jnp.where(early, e - 2, e - n_early)
-        k = jnp.where(early, f // 2, n_hop - 1 - f // (2 * n_kv))
+        k = jnp.where(early, f // 2, n_hop - 1 - f // 2)
         way = f % 2
         mine = e < 2
         slot = jnp.where(mine, own + e, way * n_hop + k)
@@ -138,50 +155,44 @@
         key_chip = jnp.where(mine, chip, lax.rem(chip + jnp.where(way == 1, hop, n_chip - hop), n_chip))
         pos0 = (key_chip * CORES + core) * keys_local + half * key_tile
         s_lo = jnp.minimum(jnp.maximum(pos0 - sub_start - span * chip - span + sub_len, 0) // sub_len, n_sub - 1)
-        return slot, key_chip, half, s_lo // RUNS
-
-    counts, ends, taken = [], [], []
+        return slot, head, key_chip, half, s_lo // RUNS
+
+    counts, ends, n_taken = [], [], []
     total = jnp.int32(0)
-    for e in range(n_early + n_late):
-        n = n_run - place(jnp.int32(e))[3]
-        if e < n_early:
-            n = n * n_kv
-            fits = jnp.int32(1) if e < 2 else (total + n <= EARLY_ITEMS).astype(jnp.int32)
-            if e > 2:
-                fits = fits * taken[-1]
-            taken.append(fits)
-            n = n * fits
-        else:
-            f = e - n_early
-            i_early = 2 + 2 * (n_hop - 1 - f // (2 * n_kv)) + f % 2
-            if i_early < n_early:
-                n = n * (1 - taken[i_early])
-        total = total + n
-        counts.append(n)
-        ends.append(total)
-
-    n_taken = taken[0]
-    for t in taken[1:]:
-        n_taken = n_taken + t
+    for head in range(n_kv):
+        base, taken = total, []
+        for e in range(n_block):
+            n = n_run - place(jnp.int32(e))[4]
+            if e < n_early:
+                fits = jnp.int32(1) if e < 2 else (total + n <= base + EARLY_ITEMS[min(head, 1)]).astype(jnp.int32)
+                taken.append(fits * taken[-1] if e > 2 else fits)
+                n = n * taken[-1]
+            else:
+                f = e - n_early
+                i_early = 2 + 2 * (n_hop - 1 - f // 2) + f % 2
+                if i_early < n_early:
+                    n = n * (1 - taken[i_early])
+            total = total + n
+            counts.append(n)
+            ends.append(total)
+        n_taken.append(sum(taken[1:], taken[0]))
 
     def following(at):
         i, e, j, n = at
         over = j + 1 >= n
-        e1 = e + 1
-        e1 = jnp.where(e1 == n_taken, n_early, e1)
-        f = e1 - n_early
-        again = (f >= 0) & (2 + 2 * (n_hop - 1 - f // (2 * n_kv)) + f % 2 < n_taken)
-        e1 = jnp.minimum(jnp.where(again, e1 + 1, e1), n_early + n_late - 1)
+        head, b = e // n_block, lax.rem(e, n_block) + 1
+        limit = n_taken[0]
+        for h in range(1, n_kv):
+            limit = jnp.where(head == h, n_taken[h], limit)
+        b = jnp.where(b == limit, n_early, b)
+        f = b - n_early
+        gone = lambda f: (f >= 0) & (2 + 2 * (n_hop - 1 - f // 2) + f % 2 < limit)
+        b = jnp.where(gone(f), jnp.where((f % 2 == 1) | gone(f + 1), n_block, b + 1), b)
+        e1 = jnp.minimum(head * n_block + b, n_kv * n_block - 1)
         e, j = jnp.where(over, e1, e), jnp.where(over, 0, j + 1)
-        slot, key_chip, half, s_lo = place(e)
-        nth = jnp.int32(0)
-        for m in range(1, n_kv):
-            nth = nth + (j >= m * (n_run - s_lo)).astype(jnp.int32)
-        head = jnp.where(e < n_early, nth, (e - n_early) // 2 % n_kv)
-        n = (n_run - s_lo) * jnp.where(e < n_early, n_kv, 1)
+        slot, head, key_chip, half, s_lo = place(e)
         i = i + 1
-        s = (s_lo + j - jnp.where(e < n_early, nth, 0) * (n_run - s_lo)) * RUNS
-        return (slot, head, s, key_chip, half, (i < total).astype(jnp.int32)), (i, e, j, n)
+        return (slot, head, (s_lo + j) * RUNS, key_chip, half, (i < total).astype(jnp.int32)), (i, e, j, n_run - s_lo)
 
     exp_scale = scale * math.log2(math.e)
     k_iota = lax.broadcasted_iota(jnp.int32, (key_tile, width), 0)
@@ -231,18 +242,6 @@
             out = out + jnp.where(e >= v, n, 0)
         return out
 
-    def gather_event(k, state):
-        goal = (EARLY_ITEMS * (k + 1)) // n_hop
-        state = advance(state, jnp.minimum(goal, end_of(jnp.minimum(2 * k + 1, n_early - 1))))
-        for way in range(2):
-            i = way * n_hop + k
-            remote(kvb.at[i], kvb.at[i], ag_send.at[i], ag_recv.at[i], nbr[way]).wait_recv()
-
-            @pl.when(k + 2 < n_hop)
-            def _():
-                remote(kvb.at[i], kvb.at[i + 2], ag_send.at[i + 2], ag_recv.at[i + 2], nbr[way]).start()
-        return state
-
     def add(dst, src, head):
         cut = key_tile // 4
 
@@ -254,11 +253,11 @@
     def partial(i, head, peer):
         return remote(acc.at[i, head], rsb.at[i, head], rs_send.at[i, head], rs_recv.at[i, head], peer)
 
-    def reduce_event(m, state):
-        k, head, way = n_hop - 1 - m // (2 * n_kv), m // 2 % n_kv, m % 2
+    def send_sums(k, way, head, state=None):
         i = way * n_hop + k
         peer = jnp.where(way == 0, left, right)
-        state = advance(state, end_of(n_early + m) + UNROLL)
+        if state is not None:
+            state = advance(state, end_of(head * n_block + n_early + 2 * (n_hop - 1 - k) + way) + UNROLL)
 
         @pl.when(k + 2 < n_hop)
         def _():
@@ -268,14 +267,55 @@
         partial(i, head, peer).start()
         return state
 
+    def arrive(k, state):
+        goal = (EARLY_ITEMS[0] * k) // (n_hop - 1)
+        state = advance(state, jnp.minimum(goal, end_of(jnp.minimum(2 * k + 1, n_early - 1))))
+        pass_on(k, 0)
+
+        @pl.when(k == max(n_hop - 3, 1))
+        def _():
+            gather_own(1)
+        return state
+
+    def both(head):
+        def trip(m, state):
+            state = lax.fori_loop(0, 2, lambda way, state: send_sums(n_hop - 1 - m, way, head, state), state)
+            base = ends[(head + 1) * n_block - 1]
+            goal = jnp.minimum(base + (EARLY_ITEMS[1] * (m + 1)) // n_hop, end_of((head + 1) * n_block + jnp.minimum(2 * m + 1, n_early - 1)))
+            state = advance(state, jnp.where(state[0] >= base, goal, state[0]))
+            pass_on(m, head + 1)
+            if head + 2 < n_kv:
+                @pl.when(m == max(n_hop - 3, 1))
+                def _():
+                    gather_own(head + 2)
+            return state
+        return trip
+
+    def settle(head):
+        for k in (1, 0):
+            for way in range(2):
+                partial(way * n_hop + k, head, nbr[1 - way]).wait_recv()
+                add(own + (k + way) % 2, way * n_hop + k, head)
+
+        @pl.loop(0, 2)
+        def _(half):
+            r = pl.ds(pl.multiple_of(half * key_tile, 8), key_tile)
+            dko[r, head, :] = acc[own + half, head, :, :head_dim] * scale
+            dvo[r, head, :] = acc[own + half, head, :, head_dim:]
+
     zero = jnp.int32(0)
     start, at = following((zero - 1, zero, zero - 1, zero + 1))
     state = (zero, (start[:3], start, at))
-    state = lax.fori_loop(0, n_hop, gather_event, state)
-    state = lax.fori_loop(0, n_late, reduce_event, state)
+    state = lax.fori_loop(1, n_hop, arrive, state)
+    for head in range(n_kv - 1):
+        state = lax.fori_loop(0, n_hop, both(head), state)
+    state = lax.fori_loop(0, 2 * n_hop - 4, lambda m, state: send_sums(n_hop - 1 - m // 2, m % 2, n_kv - 1, state), state)
+    state = advance(state, total + UNROLL)
     half_rows = lambda which: dqa.at[:, :, :, pl.ds(which * rows, rows)]
     swap = remote(half_rows(1), dqr, x_send.at[3], x_recv.at[3], sibling)
     swap.start()
+    for way in range(2):
+        send_sums(1, way, n_kv - 1)
     swap.wait_recv()
 
     @pl.loop(0, n_sub)
@@ -284,30 +324,23 @@
             x = ((dqa[h, s, :, :rows] + dqr[h, s]) * scale).astype(BF16).T
             dqo[s, :, h] = x.reshape(local_len, group, head_dim)
 
-    put_dq = pltpu.make_async_copy(dqo, dq_out, out_sem.at[0])
-    put_dq.start()
-    for head in range(n_kv):
-        for k in reversed(range(2)):
-            for way in range(2):
-                partial(way * n_hop + k, head, nbr[1 - way]).wait_recv()
-                add(own + (k + way) % 2, way * n_hop + k, head)
-
-    @pl.loop(0, 2)
-    def _(half):
-        for h in range(n_kv):
-            acc[own + half, h, :, :head_dim] = acc[own + half, h, :, :head_dim] * scale
-
-    put_kv = pltpu.make_async_copy(acc.at[pl.ds(own, 2)], dkv_out, out_sem.at[1])
-    put_kv.start()
+    puts = [pltpu.make_async_copy(a, b, out_sem.at[i]) for i, (a, b) in enumerate(((dqo, dq_out), (dko, dk_out), (dvo, dv_out)))]
+    puts[0].start()
+    for head in range(n_kv - 1):
+        settle(head)
+    for way in range(2):
+        send_sums(0, way, n_kv - 1)
+    settle(n_kv - 1)
+    puts[1].start()
+    puts[2].start()
     swap.wait_send()
     for way in range(2):
-        for j in range(n_hop):
-            i = way * n_hop + j
-            remote(kvb.at[i], kvb.at[i], ag_send.at[i], ag_recv.at[i], nbr[way]).wait_send()
+        for k in range(n_hop):
             for head in range(n_kv):
-                partial(i, head, nbr[1 - way]).wait_send()
-    put_dq.wait()
-    put_kv.wait()
+                gather(way, k, head).wait_send()
+                partial(way * n_hop + k, head, nbr[1 - way]).wait_send()
+    for c in puts:
+        c.wait()
 
 
 def solution(mesh):
@@ -333,12 +366,12 @@
         hbm = pl.BlockSpec(memory_space=pl.ANY)
         dma = pltpu.SemaphoreType.DMA
         vmem = pltpu.VMEM
-        dq, dkv = pl.pallas_call(
+        dq, dk, dv = pl.pallas_call(
             functools.partial(ring_kernel, cp_size, sub_start, head_dim ** -0.5),
             name='ring_backward',
-            out_shape=(jax.ShapeDtypeStruct(q5, BF16), jax.ShapeDtypeStruct((2, n_kv, half, 2 * head_dim), F32)),
+            out_shape=(jax.ShapeDtypeStruct(q5, BF16),) + (jax.ShapeDtypeStruct(key_act.shape, F32),) * 2,
             in_specs=[hbm] * 6,
-            out_specs=(hbm, hbm),
+            out_specs=(hbm,) * 3,
             scratch_shapes=[
                 vmem((n_slot, n_kv, half, 2 * head_dim), BF16),
                 vmem((n_slot, n_kv, half, 2 * head_dim), F32),
@@ -357,16 +390,17 @@
                 vmem((n_kv, n_sub, head_dim, CORES * rows), F32),
                 vmem((n_kv, n_sub, head_dim, rows), F32),
                 vmem(q5, BF16),
+                vmem(key_act.shape, F32),
+                vmem(key_act.shape, F32),
                 vmem((2, half, RUNS * CORES * rows), BF16),
                 vmem((2, half, RUNS * CORES * rows), BF16),
-                dma((2 * n_hop,)), dma((2 * n_hop,)), dma((2 * n_hop, n_kv)), dma((2 * n_hop, n_kv)),
-                dma((4,)), dma((4,)), dma((6,)), dma((2,)),
+                dma((2 * n_hop, n_kv)), dma((2 * n_hop, n_kv)), dma((2 * n_hop, n_kv)), dma((2 * n_hop, n_kv)),
+                dma((4,)), dma((4,)), dma((6,)), dma((3,)),
             ],
             compiler_params=pltpu.CompilerParams(collective_id=0, has_side_effects=True, vmem_limit_bytes=62 * 1024 * 1024),
             cost_estimate=pl.CostEstimate(flops=flops, bytes_accessed=30 * 2 ** 20, transcendentals=0),
         )(kv, query.reshape(q5), out_act.reshape(q5), out_grad.reshape(q5), jnp.swapaxes(row_lse, 1, 2), doc_ids.reshape(-1, LANES))
-        dkv = jnp.transpose(dkv, (0, 2, 1, 3)).reshape(keys_local, n_kv, 2 * head_dim)
-        return dq.reshape(query.shape), dkv[..., :head_dim], dkv[..., head_dim:]
+        return dq.reshape(query.shape), dk, dv
 
     return jax.shard_map(local_backward, mesh=mesh, in_specs=(q_spec, q_spec, q_spec, lse_spec, kv_spec, kv_spec, P()),
                          out_specs=(q_spec, kv_spec, kv_spec), check_vma=False)

time: 188 us -> 175 us (0.931)
  Pallas kernels: 180 us -> 168 us
    pallas_call x1, Pallas kernels: 180 us -> 168 us  [local_backward(): pl.pallas_call(functools.partial(ring_kernel, cp_size, sub_start, head_di...]
    unnamed x5 -> x7, local copies, waits for them, and re-layouts: 3.66 us -> 4.52 us
where the time goes in v4:
time: 175 us
  Pallas kernels  168 us (96%)
  local copies, waits for them, and re-layouts  5.68 us (3%)
    pallas_call x1, Pallas kernels, local_backward(): pl.pallas_call(functools.partial(ring_kernel, cp_size, sub_start, head_di...  168 us
    unnamed x7, local copies, waits for them, and re-layouts  4.52 us

profile of v4, /device:TPU:22, one launch (start us, length us, event | category | flops | bytes accessed | tf_op | source)
XLA Modules:
  0.0 175.2 jit_solution(13313182457364002050)
XLA Ops:
  0.6 1.2 copy_bitcast_fusion
  1.8 0.9 pad_maximum_fusion.kv_in
  2.7 167.9 %ring_backward.1 = (bf16[16,32,2,4,128]{4,3,2,1,0:T(4,128)(2,1)}, f32[640,2,128]{2,1,0:T(2,128)}, f32[640,2,128]{2,1,0:T(2,128)}) custom-call(bf16[2,2,320,256]{3,2,1,0:T(8,128)(2,1)} %pad_maximum_fusion.kv_in, bf16[16,32,2,4,128]{4,3,2,1,0:T(4,128)(2,1)} %bitcast.15, bf16[16,32,2,4,128]{4,3,2,1,0:T(4,128)(2,1)} %bitcast.16, ...), custom_call_target="tpu_custom_call" | custom-call | flops 46976204800 | bytes 31457280 | tf_op jit(solution)/shard_map/ring_backward/pallas_call | solution.py:369
  170.7 0.0 copy-start.1
  170.7 2.4 %copy.23 = bf16[16,32,8,128]{3,2,1,0:T(8,128)(2,1)} copy(bf16[16,32,8,128]{3,2,1,0:T(8,128)(2,1)} %bitcast.12) | data formatting | bytes 2097152
  173.0 0.0 copy-done.1
  173.0 0.0 copy-start
  173.0 0.8 copy.24
  173.9 0.5 copy-done
  174.4 0.8 copy.25
Async XLA Ops:
  170.7 2.4 %copy-start.1 = (f32[640,2,128]{2,1,0:T(2,128)S(1)}, f32[640,2,128]{2,1,0:T(2,128)}, u32[]{:S(2)}) copy-start(f32[640,2,128]{2,1,0:T(2,128)} %get-tuple-element.15) | copy-start | bytes 1966084
  173.0 1.3 copy-start

commit v5 on v4

--- a/solution.py
+++ b/solution.py
@@ -18,7 +18,7 @@
 BF16 = jnp.bfloat16
 
 
-def ring_kernel(cp_size, sub_start, scale, kv_in, q_in, o_in, do_in, lse_in, doc_in, dq_out, dk_out, dv_out,
+def ring_kernel(cp_size, sub_start, scale, k_in, v_in, q_in, o_in, do_in, lse_in, doc_in, dq_out, dk_out, dv_out,
                 kvb, acc, rsb, raw_q, raw_do, raw_o, lse, docs, qn, qt, don, dot, lines, key_doc, dqa, dqr, dqo, dko, dvo, pbuf, dsbuf,
                 ag_send, ag_recv, rs_send, rs_recv, x_send, x_recv, loc_sem, out_sem):
     n_chip = cp_size // CORES
@@ -26,7 +26,7 @@
     n_sub, local_len, n_kv, group, head_dim = q_in.shape
     rows = local_len * group
     width = CORES * rows
-    key_tile = kv_in.shape[2]
+    key_tile = k_in.shape[2]
     span = local_len * CORES
     sub_len = local_len * cp_size
     keys_local = 2 * key_tile
@@ -52,10 +52,15 @@
         i = way * n_hop + k
         return remote(kvb.at[i, head] if src is None else src, kvb.at[i, head], ag_send.at[i, head], ag_recv.at[i, head], nbr[way])
 
+    def sides(ref):
+        return (ref.at[:, pl.ds(0, head_dim)], ref.at[:, pl.ds(head_dim, head_dim)])
+
     def gather_own(head):
         for j in range(2):
             for way in range(2):
-                gather(way, j, head, kv_in.at[(j + way) % 2, head]).start()
+                i = way * n_hop + j
+                for src, dst in zip((k_in, v_in), sides(kvb.at[i, head])):
+                    remote(src.at[(j + way) % 2, head], dst, ag_send.at[i, head], ag_recv.at[i, head], nbr[way]).start()
 
     def pass_on(k, head):
         for way in range(2):
@@ -70,7 +75,8 @@
     share = [remote(q_in, raw_q.at[1], x_send.at[0], x_recv.at[0], sibling),
              remote(do_in, raw_do.at[1], x_send.at[1], x_recv.at[1], sibling)]
     local = [pltpu.make_async_copy(a, b, loc_sem.at[i]) for i, (a, b) in enumerate((
-        (doc_in, docs), (lse_in, lse), (do_in, raw_do.at[0]), (o_in, raw_o), (q_in, raw_q.at[0]), (kv_in, kvb.at[pl.ds(own, 2)])))]
+        (doc_in, docs), (lse_in, lse), (do_in, raw_do.at[0]), (o_in, raw_o), (q_in, raw_q.at[0]),
+        (k_in, kvb.at[pl.ds(own, 2), :, :, pl.ds(0, head_dim)]), (v_in, kvb.at[pl.ds(own, 2), :, :, pl.ds(head_dim, head_dim)])))]
     for c in local + share:
         c.start()
 
@@ -300,7 +306,7 @@
         @pl.loop(0, 2)
         def _(half):
             r = pl.ds(pl.multiple_of(half * key_tile, 8), key_tile)
-            dko[r, head, :] = acc[own + half, head, :, :head_dim] * scale
+            dko[r, head, :] = acc[own + half, head, :, :head_dim]
             dvo[r, head, :] = acc[own + half, head, :, head_dim:]
 
     zero = jnp.int32(0)
@@ -321,7 +327,7 @@
     @pl.loop(0, n_sub)
     def _(s):
         for h in range(n_kv):
-            x = ((dqa[h, s, :, :rows] + dqr[h, s]) * scale).astype(BF16).T
+            x = (dqa[h, s, :, :rows] + dqr[h, s]).T
             dqo[s, :, h] = x.reshape(local_len, group, head_dim)
 
     puts = [pltpu.make_async_copy(a, b, out_sem.at[i]) for i, (a, b) in enumerate(((dqo, dq_out), (dko, dk_out), (dvo, dv_out)))]
@@ -361,16 +367,16 @@
         n_slot = 2 * n_hop + 2
         q5 = (n_sub, local_len, n_kv, group, head_dim)
         cut = lambda x: jnp.transpose(x.reshape(2, half, n_kv, head_dim), (0, 2, 1, 3))
-        kv = jnp.concatenate([cut(key_act), cut(value_act)], axis=-1)
+        scale = head_dim ** -0.5
         flops = 2 * 5 * n_kv * n_sub * 2 * rows * head_dim * keys_local * n_hop
         hbm = pl.BlockSpec(memory_space=pl.ANY)
         dma = pltpu.SemaphoreType.DMA
         vmem = pltpu.VMEM
         dq, dk, dv = pl.pallas_call(
-            functools.partial(ring_kernel, cp_size, sub_start, head_dim ** -0.5),
+            functools.partial(ring_kernel, cp_size, sub_start, scale),
             name='ring_backward',
-            out_shape=(jax.ShapeDtypeStruct(q5, BF16),) + (jax.ShapeDtypeStruct(key_act.shape, F32),) * 2,
-            in_specs=[hbm] * 6,
+            out_shape=(jax.ShapeDtypeStruct(q5, F32),) + (jax.ShapeDtypeStruct(key_act.shape, F32),) * 2,
+            in_specs=[hbm] * 7,
             out_specs=(hbm,) * 3,
             scratch_shapes=[
                 vmem((n_slot, n_kv, half, 2 * head_dim), BF16),
@@ -389,18 +395,18 @@
                 vmem((n_chip, keys_local, LANES), jnp.int32),
                 vmem((n_kv, n_sub, head_dim, CORES * rows), F32),
                 vmem((n_kv, n_sub, head_dim, rows), F32),
-                vmem(q5, BF16),
+                vmem(q5, F32),
                 vmem(key_act.shape, F32),
                 vmem(key_act.shape, F32),
                 vmem((2, half, RUNS * CORES * rows), BF16),
                 vmem((2, half, RUNS * CORES * rows), BF16),
                 dma((2 * n_hop, n_kv)), dma((2 * n_hop, n_kv)), dma((2 * n_hop, n_kv)), dma((2 * n_hop, n_kv)),
-                dma((4,)), dma((4,)), dma((6,)), dma((3,)),
+                dma((4,)), dma((4,)), dma((7,)), dma((3,)),
             ],
-            compiler_params=pltpu.CompilerParams(collective_id=0, has_side_effects=True, vmem_limit_bytes=62 * 1024 * 1024),
+            compiler_params=pltpu.CompilerParams(collective_id=0, has_side_effects=True, vmem_limit_bytes=52 * 1024 * 1024),
             cost_estimate=pl.CostEstimate(flops=flops, bytes_accessed=30 * 2 ** 20, transcendentals=0),
-        )(kv, query.reshape(q5), out_act.reshape(q5), out_grad.reshape(q5), jnp.swapaxes(row_lse, 1, 2), doc_ids.reshape(-1, LANES))
-        return dq.reshape(query.shape), dk, dv
+        )(cut(key_act), cut(value_act), query.reshape(q5), out_act.reshape(q5), out_grad.reshape(q5), jnp.swapaxes(row_lse, 1, 2), doc_ids.reshape(-1, LANES))
+        return (dq.reshape(query.shape) * scale).astype(BF16), dk * scale, dv
 
     return jax.shard_map(local_backward, mesh=mesh, in_specs=(q_spec, q_spec, q_spec, lse_spec, kv_spec, kv_spec, P()),
                          out_specs=(q_spec, kv_spec, kv_spec), check_vma=False)

time: 175 us -> 177 us (1.011)
  other arithmetic: 0.91 us -> 4.38 us
  local copies, waits for them, and re-layouts: 5.68 us -> 3.61 us
    convert_element_type x0 -> x1, other arithmetic: none -> 3.2 us  [local_backward(): return ((dq.reshape(query.shape) * scale).astype(BF16), dk * scale, dv)]
    unnamed x7, local copies, waits for them, and re-layouts: 4.52 us -> 2.45 us
where the time goes in v5:
time: 177 us
  Pallas kernels  168 us (95%)
  other arithmetic  4.38 us (2%)
  local copies, waits for them, and re-layouts  3.61 us (2%)
    pallas_call x1, Pallas kernels, local_backward(): pl.pallas_call(functools.partial(ring_kernel, cp_size, sub_start, scale),...  168 us

profile of v5, /device:TPU:22, one launch (start us, length us, event | category | flops | bytes accessed | tf_op | source)
XLA Modules:
  0.0 177.0 jit_solution(17891276796338397611)
XLA Ops:
  0.6 1.2 copy_bitcast_fusion
  1.8 0.0 copy-start
  1.8 0.8 copy-done
  2.6 0.0 copy-start.1
  2.6 0.8 copy-done.1
  3.4 168.3 %ring_backward.1 = (f32[16,32,2,4,128]{4,3,2,1,0:T(4,128)}, f32[640,2,128]{2,1,0:T(2,128)S(1)}, f32[640,2,128]{2,1,0:T(2,128)}) custom-call(bf16[2,2,320,128]{3,2,1,0:T(8,128)(2,1)S(1)} %get-tuple-element.10.k_in, bf16[2,2,320,128]{3,2,1,0:T(8,128)(2,1)S(1)} %get-tuple-element.9.v_in, bf16[16,32,2,4,128]{4,3,2,1,0:T(4,128)(2,1)} %bitcast.17, ...), custom_call_target="tpu_custom_call" | custom-call | flops 46976204800 | bytes 31457280 | tf_op jit(solution)/shard_map/ring_backward/pallas_call | solution.py:375
  171.7 0.0 copy-start.2
  171.8 3.2 %multiply_convert_fusion = bf16[16,32,2,4,128]{4,3,2,1,0:T(4,128)(2,1)} fusion(f32[16,32,2,4,128]{4,3,2,1,0:T(4,128)} %get-tuple-element.6), kind=kLoop, calls=%fused_computation | loop fusion | flops 1048576 | bytes 3145728 | tf_op jit(solution)/shard_map/convert_element_type | solution.py:409
  175.0 1.2 broadcast_multiply_fusion
  176.1 0.0 copy-done.2
  176.1 0.8 copy.21
Async XLA Ops:
  1.8 0.8 copy-start
  2.6 0.8 copy-start.1
  171.7 4.4 %copy-start.2 = (f32[640,2,128]{2,1,0:T(2,128)S(1)}, f32[640,2,128]{2,1,0:T(2,128)}, u32[]{:S(2)}) copy-start(f32[640,2,128]{2,1,0:T(2,128)} %get-tuple-element.16) | copy-start | bytes 1966084

commit v6 on v5

--- a/solution.py
+++ b/solution.py
@@ -19,7 +19,7 @@
 
 
 def ring_kernel(cp_size, sub_start, scale, k_in, v_in, q_in, o_in, do_in, lse_in, doc_in, dq_out, dk_out, dv_out,
-                kvb, acc, rsb, raw_q, raw_do, raw_o, lse, docs, qn, qt, don, dot, lines, key_doc, dqa, dqr, dqo, dko, dvo, pbuf, dsbuf,
+                kvb, acc, rsb, raw_q, raw_do, raw_o, lse, docs, qn, qt, don, dot, lines, key_doc, dqa, dqr, dko, dvo, pbuf, dsbuf,
                 ag_send, ag_recv, rs_send, rs_recv, x_send, x_recv, loc_sem, out_sem):
     n_chip = cp_size // CORES
     n_hop = n_chip - 1
@@ -306,7 +306,7 @@
         @pl.loop(0, 2)
         def _(half):
             r = pl.ds(pl.multiple_of(half * key_tile, 8), key_tile)
-            dko[r, head, :] = acc[own + half, head, :, :head_dim]
+            dko[r, head, :] = acc[own + half, head, :, :head_dim] * scale
             dvo[r, head, :] = acc[own + half, head, :, head_dim:]
 
     zero = jnp.int32(0)
@@ -327,10 +327,10 @@
     @pl.loop(0, n_sub)
     def _(s):
         for h in range(n_kv):
-            x = (dqa[h, s, :, :rows] + dqr[h, s]).T
-            dqo[s, :, h] = x.reshape(local_len, group, head_dim)
-
-    puts = [pltpu.make_async_copy(a, b, out_sem.at[i]) for i, (a, b) in enumerate(((dqo, dq_out), (dko, dk_out), (dvo, dv_out)))]
+            x = ((dqa[h, s, :, :rows] + dqr[h, s]) * scale).astype(BF16).T
+            raw_q[0, s, :, h] = x.reshape(local_len, group, head_dim)
+
+    puts = [pltpu.make_async_copy(a, b, out_sem.at[i]) for i, (a, b) in enumerate(((raw_q.at[0], dq_out), (dko, dk_out), (dvo, dv_out)))]
     puts[0].start()
     for head in range(n_kv - 1):
         settle(head)
@@ -347,6 +347,18 @@
                 partial(way * n_hop + k, head, nbr[1 - way]).wait_send()
     for c in puts:
         c.wait()
+
+
+def copy_kernel(a, b, c, a_out, b_out, c_out, a_buf, b_buf, c_buf, in_sem, out_sem):
+    ins = [pltpu.make_async_copy(x, y, in_sem.at[i]) for i, (x, y) in enumerate(((a, a_buf), (b, b_buf), (c, c_buf)))]
+    outs = [pltpu.make_async_copy(x, y, out_sem.at[i]) for i, (x, y) in enumerate(((a_buf, a_out), (b_buf, b_out), (c_buf, c_out)))]
+    for x in ins:
+        x.start()
+    for x, y in zip(ins, outs):
+        x.wait()
+        y.start()
+    for y in outs:
+        y.wait()
 
 
 def solution(mesh):
@@ -375,7 +387,7 @@
         dq, dk, dv = pl.pallas_call(
             functools.partial(ring_kernel, cp_size, sub_start, scale),
             name='ring_backward',
-            out_shape=(jax.ShapeDtypeStruct(q5, F32),) + (jax.ShapeDtypeStruct(key_act.shape, F32),) * 2,
+            out_shape=(jax.ShapeDtypeStruct(q5, BF16),) + (jax.ShapeDtypeStruct(key_act.shape, F32),) * 2,
             in_specs=[hbm] * 7,
             out_specs=(hbm,) * 3,
             scratch_shapes=[
@@ -395,7 +407,6 @@
                 vmem((n_chip, keys_local, LANES), jnp.int32),
                 vmem((n_kv, n_sub, head_dim, CORES * rows), F32),
                 vmem((n_kv, n_sub, head_dim, rows), F32),
-                vmem(q5, F32),
                 vmem(key_act.shape, F32),
                 vmem(key_act.shape, F32),
                 vmem((2, half, RUNS * CORES * rows), BF16),
@@ -403,10 +414,19 @@
                 dma((2 * n_hop, n_kv)), dma((2 * n_hop, n_kv)), dma((2 * n_hop, n_kv)), dma((2 * n_hop, n_kv)),
                 dma((4,)), dma((4,)), dma((7,)), dma((3,)),
             ],
-            compiler_params=pltpu.CompilerParams(collective_id=0, has_side_effects=True, vmem_limit_bytes=52 * 1024 * 1024),
+            compiler_params=pltpu.CompilerParams(collective_id=0, has_side_effects=True, vmem_limit_bytes=62 * 1024 * 1024),
             cost_estimate=pl.CostEstimate(flops=flops, bytes_accessed=30 * 2 ** 20, transcendentals=0),
         )(cut(key_act), cut(value_act), query.reshape(q5), out_act.reshape(q5), out_grad.reshape(q5), jnp.swapaxes(row_lse, 1, 2), doc_ids.reshape(-1, LANES))
-        return (dq.reshape(query.shape) * scale).astype(BF16), dk * scale, dv
+        dq, dk, dv = pl.pallas_call(
+            copy_kernel,
+            name='results',
+            out_shape=tuple(jax.ShapeDtypeStruct(x.shape, x.dtype) for x in (dq, dk, dv)),
+            in_specs=[hbm] * 3,
+            out_specs=(hbm,) * 3,
+            scratch_shapes=[vmem(x.shape, x.dtype) for x in (dq, dk, dv)] + [dma((3,)), dma((3,))],
+            cost_estimate=pl.CostEstimate(flops=0, bytes_accessed=2 ** 22, transcendentals=0),
+        )(dq, dk, dv)
+        return dq.reshape(query.shape), dk, dv
 
     return jax.shard_map(local_backward, mesh=mesh, in_specs=(q_spec, q_spec, q_spec, lse_spec, kv_spec, kv_spec, P()),
                          out_specs=(q_spec, kv_spec, kv_spec), check_vma=False)

time: 177 us -> 173 us (0.977)
  other arithmetic: 4.38 us -> 0 us
  Pallas kernels: 168 us -> 171 us
    convert_element_type x1 -> x0, other arithmetic: 3.2 us -> none  [local_backward(): return ((dq.reshape(query.shape) * scale).astype(BF16), dk * scale, dv)]
    pallas_call x0 -> x1, Pallas kernels: none -> 2.67 us  [local_backward(): pl.pallas_call(copy_kernel, name='results', out_shape=tuple((jax.ShapeDty...]
    unnamed x7 -> x0, local copies, waits for them, and re-layouts: 2.45 us -> none
where the time goes in v6:
time: 173 us
  Pallas kernels  171 us (99%)
  local copies, waits for them, and re-layouts  1.99 us (1%)
    pallas_call x1, Pallas kernels, local_backward(): pl.pallas_call(functools.partial(ring_kernel, cp_size, sub_start, scale),...  168 us

profile of v6, /device:TPU:22, one launch (start us, length us, event | category | flops | bytes accessed | tf_op | source)
XLA Modules:
  0.0 173.3 jit_solution(13366598838371742327)
XLA Ops:
  0.6 2.0 %copy_bitcast_fusion = (bf16[2,2,320,128]{3,2,1,0:T(8,128)(2,1)}, bf16[2,2,320,128]{3,2,1,0:T(8,128)(2,1)}) fusion(bf16[2,320,2,128]{3,2,1,0:T(2,128)(2,1)} %bitcast.12, bf16[2,320,2,128]{3,2,1,0:T(2,128)(2,1)} %bitcast.13), kind=kLoop, calls=%fused_computation | loop fusion | bytes 1310720 | tf_op jit(solution)/shard_map/transpose | solution.py:381
  2.6 168.0 %ring_backward.1 = (bf16[16,32,2,4,128]{4,3,2,1,0:T(4,128)(2,1)}, f32[640,2,128]{2,1,0:T(2,128)}, f32[640,2,128]{2,1,0:T(2,128)}) custom-call(bf16[2,2,320,128]{3,2,1,0:T(8,128)(2,1)} %get-tuple-element.16.k_in, bf16[2,2,320,128]{3,2,1,0:T(8,128)(2,1)} %get-tuple-element.15.v_in, bf16[16,32,2,4,128]{4,3,2,1,0:T(4,128)(2,1)} %bitcast.14, ...), custom_call_target="tpu_custom_call" | custom-call | flops 46976204800 | bytes 31457280 | tf_op jit(solution)/shard_map/ring_backward/pallas_call | solution.py:387
  170.6 2.7 %results.1 = (bf16[16,32,2,4,128]{4,3,2,1,0:T(4,128)(2,1)}, f32[640,2,128]{2,1,0:T(2,128)}, f32[640,2,128]{2,1,0:T(2,128)}) custom-call(bf16[16,32,2,4,128]{4,3,2,1,0:T(4,128)(2,1)} %get-tuple-element.9.a, f32[640,2,128]{2,1,0:T(2,128)} %get-tuple-element.10.b, f32[640,2,128]{2,1,0:T(2,128)} %get-tuple-element.11.c), custom_call_target="tpu_custom_call" | custom-call | bytes 4194304 | tf_op jit(solution)/shard_map/results/pallas_call | solution.py:420

commit v7 on v6

--- a/solution.py
+++ b/solution.py
@@ -11,22 +11,23 @@
 MESH = pl.DeviceIdType.MESH
 CORES = 2
 LANES = 128
+SPLIT = 64
 RUNS = 2
 UNROLL = 2
-EARLY_ITEMS = (36, 40)
+EARLY_ITEMS = (26, 20)
 F32 = jnp.float32
 BF16 = jnp.bfloat16
 
 
 def ring_kernel(cp_size, sub_start, scale, k_in, v_in, q_in, o_in, do_in, lse_in, doc_in, dq_out, dk_out, dv_out,
-                kvb, acc, rsb, raw_q, raw_do, raw_o, lse, docs, qn, qt, don, dot, lines, key_doc, dqa, dqr, dko, dvo, pbuf, dsbuf,
+                kvb, acc, rsb, raw_q, raw_do, raw_o, lse, docs, qn, qt, don, dot, lines, key_doc, dqa, dqr, dko, dvo, pbuf, dsbuf, raw_kv,
                 ag_send, ag_recv, rs_send, rs_recv, x_send, x_recv, loc_sem, out_sem):
     n_chip = cp_size // CORES
     n_hop = n_chip - 1
     n_sub, local_len, n_kv, group, head_dim = q_in.shape
     rows = local_len * group
     width = CORES * rows
-    key_tile = k_in.shape[2]
+    key_tile = k_in.shape[0] // 2
     span = local_len * CORES
     sub_len = local_len * cp_size
     keys_local = 2 * key_tile
@@ -42,6 +43,29 @@
     barrier = pltpu.get_barrier_semaphore()
     for peer in (right, left, sibling):
         pl.semaphore_signal(barrier, inc=1, device_id={'cp': peer}, device_id_type=MESH)
+
+    own_kv = [pltpu.make_async_copy(x, raw_kv.at[i], loc_sem.at[5 + i]) for i, x in enumerate((k_in, v_in))]
+    local = [pltpu.make_async_copy(a, b, loc_sem.at[i]) for i, (a, b) in enumerate((
+        (doc_in, docs), (lse_in, lse), (do_in, raw_do.at[0]), (o_in, raw_o), (q_in, raw_q.at[0])))]
+    for c in own_kv + local:
+        c.start()
+
+    @pl.loop(0, n_sub)
+    def _(s):
+        for h in range(n_kv):
+            dqa[h, s] = jnp.zeros(dqa.shape[2:], F32)
+
+    for c in own_kv:
+        c.wait()
+    for half in range(2):
+        @pl.loop(0, key_tile // SPLIT)
+        def _(i):
+            r = pl.multiple_of(i * SPLIT, SPLIT)
+            for part in range(2):
+                x = raw_kv[part, pl.ds(half * key_tile + r, SPLIT)].astype(F32)
+                for h in range(n_kv):
+                    kvb[own + half, h, pl.ds(r, SPLIT), part * head_dim:(part + 1) * head_dim] = x[:, h].astype(BF16)
+
     pl.semaphore_wait(barrier, 3)
 
     def remote(src, dst, send, recv, peer):
@@ -52,15 +76,10 @@
         i = way * n_hop + k
         return remote(kvb.at[i, head] if src is None else src, kvb.at[i, head], ag_send.at[i, head], ag_recv.at[i, head], nbr[way])
 
-    def sides(ref):
-        return (ref.at[:, pl.ds(0, head_dim)], ref.at[:, pl.ds(head_dim, head_dim)])
-
     def gather_own(head):
         for j in range(2):
             for way in range(2):
-                i = way * n_hop + j
-                for src, dst in zip((k_in, v_in), sides(kvb.at[i, head])):
-                    remote(src.at[(j + way) % 2, head], dst, ag_send.at[i, head], ag_recv.at[i, head], nbr[way]).start()
+                gather(way, j, head, kvb.at[own + (j + way) % 2, head]).start()
 
     def pass_on(k, head):
         for way in range(2):
@@ -74,21 +93,13 @@
     gather_own(0)
     share = [remote(q_in, raw_q.at[1], x_send.at[0], x_recv.at[0], sibling),
              remote(do_in, raw_do.at[1], x_send.at[1], x_recv.at[1], sibling)]
-    local = [pltpu.make_async_copy(a, b, loc_sem.at[i]) for i, (a, b) in enumerate((
-        (doc_in, docs), (lse_in, lse), (do_in, raw_do.at[0]), (o_in, raw_o), (q_in, raw_q.at[0]),
-        (k_in, kvb.at[pl.ds(own, 2), :, :, pl.ds(0, head_dim)]), (v_in, kvb.at[pl.ds(own, 2), :, :, pl.ds(head_dim, head_dim)])))]
-    for c in local + share:
+    for c in share:
         c.start()
 
     def mine(which):
         return lines.at[:, :, :, pl.ds(which * rows, rows)]
 
     share_lines = remote(mine(0), mine(1), x_send.at[2], x_recv.at[2], sibling)
-
-    @pl.loop(0, n_sub)
-    def _(s):
-        for h in range(n_kv):
-            dqa[h, s] = jnp.zeros(dqa.shape[2:], F32)
 
     @pl.loop(0, acc.shape[0])
     def _(i):
@@ -378,7 +389,6 @@
         n_hop = n_chip - 1
         n_slot = 2 * n_hop + 2
         q5 = (n_sub, local_len, n_kv, group, head_dim)
-        cut = lambda x: jnp.transpose(x.reshape(2, half, n_kv, head_dim), (0, 2, 1, 3))
         scale = head_dim ** -0.5
         flops = 2 * 5 * n_kv * n_sub * 2 * rows * head_dim * keys_local * n_hop
         hbm = pl.BlockSpec(memory_space=pl.ANY)
@@ -411,12 +421,13 @@
                 vmem(key_act.shape, F32),
                 vmem((2, half, RUNS * CORES * rows), BF16),
                 vmem((2, half, RUNS * CORES * rows), BF16),
+                vmem((2,) + key_act.shape, BF16),
                 dma((2 * n_hop, n_kv)), dma((2 * n_hop, n_kv)), dma((2 * n_hop, n_kv)), dma((2 * n_hop, n_kv)),
                 dma((4,)), dma((4,)), dma((7,)), dma((3,)),
             ],
             compiler_params=pltpu.CompilerParams(collective_id=0, has_side_effects=True, vmem_limit_bytes=62 * 1024 * 1024),
             cost_estimate=pl.CostEstimate(flops=flops, bytes_accessed=30 * 2 ** 20, transcendentals=0),
-        )(cut(key_act), cut(value_act), query.reshape(q5), out_act.reshape(q5), out_grad.reshape(q5), jnp.swapaxes(row_lse, 1, 2), doc_ids.reshape(-1, LANES))
+        )(key_act, value_act, query.reshape(q5), out_act.reshape(q5), out_grad.reshape(q5), jnp.swapaxes(row_lse, 1, 2), doc_ids.reshape(-1, LANES))
         dq, dk, dv = pl.pallas_call(
             copy_kernel,
             name='results',

time: 173 us -> 175 us (1.012); the launches traced: 173 us -> 172 us
  local copies, waits for them, and re-layouts: 1.99 us -> 0 us
    transpose x1 -> x0, local copies, waits for them, and re-layouts: 1.99 us -> none  [local_backward(): jnp.transpose(x.reshape(2, half, n_kv, head_dim), (0, 2, 1, 3))]
where the time goes in v7:
time: 175 us; the launch traced here: 172 us
  Pallas kernels  171 us (98%)
    pallas_call x1, Pallas kernels, local_backward(): pl.pallas_call(functools.partial(ring_kernel, cp_size, sub_start, scale),...  169 us

profile of v7, /device:TPU:22, one launch (start us, length us, event | category | flops | bytes accessed | tf_op | source)
XLA Modules:
  0.0 172.0 jit_solution(2227382410661682981)
XLA Ops:
  0.6 168.7 %ring_backward.1 = (bf16[16,32,2,4,128]{4,3,2,1,0:T(4,128)(2,1)}, f32[640,2,128]{2,1,0:T(2,128)}, f32[640,2,128]{2,1,0:T(2,128)}) custom-call(bf16[640,2,128]{2,1,0:T(2,128)(2,1)} %k_in.1, bf16[640,2,128]{2,1,0:T(2,128)(2,1)} %v_in.1, bf16[16,32,2,4,128]{4,3,2,1,0:T(4,128)(2,1)} %bitcast.6, bf16[16,32,2,4,128]{4,3,2,1,0:T(4,128)(2,1)} %bitcast.7, ...), custom_call_target="tpu_custom_call" | custom-call | flops 46976204800 | bytes 31457280 | tf_op jit(solution)/shard_map/ring_backward/pallas_call | solution.py:397
  169.3 2.7 %results.1 = (bf16[16,32,2,4,128]{4,3,2,1,0:T(4,128)(2,1)}, f32[640,2,128]{2,1,0:T(2,128)}, f32[640,2,128]{2,1,0:T(2,128)}) custom-call(bf16[16,32,2,4,128]{4,3,2,1,0:T(4,128)(2,1)} %get-tuple-element.9.a, f32[640,2,128]{2,1,0:T(2,128)} %get-tuple-element.10.b, f32[640,2,128]{2,1,0:T(2,128)} %get-tuple-element.11.c), custom_call_target="tpu_custom_call" | custom-call | bytes 4194304 | tf_op jit(solution)/shard_map/results/pallas_call | solution.py:431

commit v8 on v7

--- a/solution.py
+++ b/solution.py
@@ -14,7 +14,7 @@
 SPLIT = 64
 RUNS = 2
 UNROLL = 2
-EARLY_ITEMS = (26, 20)
+EARLY_ITEMS = (26, 16)
 F32 = jnp.float32
 BF16 = jnp.bfloat16
 
@@ -326,13 +326,13 @@
     state = lax.fori_loop(1, n_hop, arrive, state)
     for head in range(n_kv - 1):
         state = lax.fori_loop(0, n_hop, both(head), state)
-    state = lax.fori_loop(0, 2 * n_hop - 4, lambda m, state: send_sums(n_hop - 1 - m // 2, m % 2, n_kv - 1, state), state)
+    state = lax.fori_loop(0, 2 * n_hop - 2, lambda m, state: send_sums(n_hop - 1 - m // 2, m % 2, n_kv - 1, state), state)
     state = advance(state, total + UNROLL)
     half_rows = lambda which: dqa.at[:, :, :, pl.ds(which * rows, rows)]
     swap = remote(half_rows(1), dqr, x_send.at[3], x_recv.at[3], sibling)
     swap.start()
     for way in range(2):
-        send_sums(1, way, n_kv - 1)
+        send_sums(0, way, n_kv - 1)
     swap.wait_recv()
 
     @pl.loop(0, n_sub)
@@ -343,11 +343,8 @@
 
     puts = [pltpu.make_async_copy(a, b, out_sem.at[i]) for i, (a, b) in enumerate(((raw_q.at[0], dq_out), (dko, dk_out), (dvo, dv_out)))]
     puts[0].start()
-    for head in range(n_kv - 1):
+    for head in range(n_kv):
         settle(head)
-    for way in range(2):
-        send_sums(0, way, n_kv - 1)
-    settle(n_kv - 1)
     puts[1].start()
     puts[2].start()
     swap.wait_send()

time: 175 us -> 170 us (0.971); the launches traced: 172 us -> 170 us
  Pallas kernels: 171 us -> 169 us
    pallas_call x1, Pallas kernels: 169 us -> 166 us  [local_backward(): pl.pallas_call(functools.partial(ring_kernel, cp_size, sub_start, scale),...]
where the time goes in v8:
time: 170 us
  Pallas kernels  169 us (99%)
    pallas_call x1, Pallas kernels, local_backward(): pl.pallas_call(functools.partial(ring_kernel, cp_size, sub_start, scale),...  166 us

profile of v8, /device:TPU:22, one launch (start us, length us, event | category | flops | bytes accessed | tf_op | source)
XLA Modules:
  0.0 169.8 jit_solution(10286818146710817971)
XLA Ops:
  0.6 166.4 %ring_backward.1 = (bf16[16,32,2,4,128]{4,3,2,1,0:T(4,128)(2,1)}, f32[640,2,128]{2,1,0:T(2,128)}, f32[640,2,128]{2,1,0:T(2,128)}) custom-call(bf16[640,2,128]{2,1,0:T(2,128)(2,1)} %k_in.1, bf16[640,2,128]{2,1,0:T(2,128)(2,1)} %v_in.1, bf16[16,32,2,4,128]{4,3,2,1,0:T(4,128)(2,1)} %bitcast.6, bf16[16,32,2,4,128]{4,3,2,1,0:T(4,128)(2,1)} %bitcast.7, ...), custom_call_target="tpu_custom_call" | custom-call | flops 46976204800 | bytes 31457280 | tf_op jit(solution)/shard_map/ring_backward/pallas_call | solution.py:394
  167.1 2.7 %results.1 = (bf16[16,32,2,4,128]{4,3,2,1,0:T(4,128)(2,1)}, f32[640,2,128]{2,1,0:T(2,128)}, f32[640,2,128]{2,1,0:T(2,128)}) custom-call(bf16[16,32,2,4,128]{4,3,2,1,0:T(4,128)(2,1)} %get-tuple-element.9.a, f32[640,2,128]{2,1,0:T(2,128)} %get-tuple-element.10.b, f32[640,2,128]{2,1,0:T(2,128)} %get-tuple-element.11.c), custom_call_target="tpu_custom_call" | custom-call | bytes 4194304 | tf_op jit(solution)/shard_map/results/pallas_call | solution.py:428

commit v9 on v8

--- a/solution.py
+++ b/solution.py
@@ -14,7 +14,9 @@
 SPLIT = 64
 RUNS = 2
 UNROLL = 2
-EARLY_ITEMS = (26, 16)
+EARLY_ITEMS = 26
+ORDER = ('e1 W4 e2 W4 e3 W4 e4 O W4 e5 W4 e6 R60 R61 E0 R50 R51 E1 R40 R41 E2 R30 R31 E3 R20 R21 E4 R10 R11 E5 R00 R01 E6 '
+         'T60 T61 T50 T51 T40 T41 T30 T31 T20 T21 T10 T11 F T00 T01')
 F32 = jnp.float32
 BF16 = jnp.bfloat16
 
@@ -111,40 +113,46 @@
     local[0].wait()
     tiles = keys_local // LANES
 
-    @pl.loop(0, n_chip * tiles)
-    def _(i):
-        b, r = i // tiles, lax.rem(i, tiles)
-        row = (b * CORES + core) * tiles + r
-        key_doc[b, pl.ds(pl.multiple_of(r * LANES, LANES), LANES), :] = jnp.broadcast_to(docs[pl.ds(row, 1), :], (LANES, LANES)).T
+    @pl.loop(0, n_chip)
+    def _(b):
+        for r in range(tiles):
+            row = docs[pl.ds((b * CORES + core) * tiles + r, 1), :]
+            key_doc[b, r * LANES:(r + 1) * LANES, :] = jnp.broadcast_to(row, (LANES, LANES)).T
 
     lane = lax.broadcasted_iota(jnp.int32, (8, rows), 1)
     sub = lax.broadcasted_iota(jnp.int32, (8, rows), 0)
     for c in local[1:4]:
         c.wait()
 
-    @pl.loop(0, n_sub)
-    def _(s):
-        rep = jnp.concatenate([lse[s]] * (LANES // local_len), axis=1)
-        wide = jnp.take_along_axis(rep, lane // group, axis=1)
-        for h in range(n_kv):
-            line = jnp.sum(jnp.where(sub - group * h == lane % group, wide, 0.0), axis=0, keepdims=True) * math.log2(math.e)
-            prod = raw_do[0, s, :, h].reshape(rows, head_dim).astype(F32) * raw_o[s, :, h].reshape(rows, head_dim).astype(F32)
-            total = jnp.broadcast_to(jnp.sum(prod, axis=1, keepdims=True), (rows, LANES)).T
-            first = sub_start + s * sub_len + me * local_len
-            doc_row = jnp.broadcast_to(docs[pl.ds(first // LANES, 1), :], (8, LANES))
-            doc = jnp.take_along_axis(doc_row, lax.rem(first, LANES) + lane // group, axis=1).astype(F32)
-            lines[h, s, :, :rows] = jnp.where(sub == 0, line, jnp.where(sub == 1, total[:8, :], doc))
+    side = math.gcd(n_sub, 4)
+
+    @pl.loop(0, n_sub // side)
+    def _(t):
+        for u in range(side):
+            s = t * side + u
+            rep = jnp.concatenate([lse[s]] * (LANES // local_len), axis=1)
+            wide = jnp.take_along_axis(rep, lane // group, axis=1)
+            for h in range(n_kv):
+                line = jnp.sum(jnp.where(sub - group * h == lane % group, wide, 0.0), axis=0, keepdims=True) * math.log2(math.e)
+                prod = raw_do[0, s, :, h].reshape(rows, head_dim).astype(F32) * raw_o[s, :, h].reshape(rows, head_dim).astype(F32)
+                total = jnp.broadcast_to(jnp.sum(prod, axis=1, keepdims=True), (rows, LANES)).T
+                first = sub_start + s * sub_len + me * local_len
+                doc_row = jnp.broadcast_to(docs[pl.ds(first // LANES, 1), :], (8, LANES))
+                doc = jnp.take_along_axis(doc_row, lax.rem(first, LANES) + lane // group, axis=1).astype(F32)
+                lines[h, s, :, :rows] = jnp.where(sub == 0, line, jnp.where(sub == 1, total[:8, :], doc))
 
     share_lines.start()
 
     def spread(c):
-        @pl.loop(0, n_sub)
-        def _(s):
-            for h in range(n_kv):
-                for raw, nat, tr in ((raw_q, qn, qt), (raw_do, don, dot)):
-                    x = raw[c, s, :, h].reshape(rows, head_dim)
-                    nat[h, s, c * rows:(c + 1) * rows, :] = x
-                    tr[h, s, :, c * rows:(c + 1) * rows] = x.T
+        @pl.loop(0, n_sub // RUNS)
+        def _(t):
+            for u in range(RUNS):
+                s = t * RUNS + u
+                for h in range(n_kv):
+                    for raw, nat, tr in ((raw_q, qn, qt), (raw_do, don, dot)):
+                        x = raw[c, s, :, h].reshape(rows, head_dim)
+                        nat[h, s, c * rows:(c + 1) * rows, :] = x
+                        tr[h, s, :, c * rows:(c + 1) * rows] = x.T
 
     for c in local[4:]:
         c.wait()
@@ -157,55 +165,58 @@
 
     n_run = n_sub // RUNS
     n_early = 2 + min(8, 2 * n_hop)
-    n_block = n_early + 2 * n_hop
+    n_first = n_early + 2 * n_hop
+    n_block = 2 * n_hop + 2
+    n_entry = n_first + (n_kv - 1) * n_block
 
     def place(e):
-        head, e = e // n_block, lax.rem(e, n_block)
-        early = e < n_early
-        f = jnp.where(early, e - 2, e - n_early)
-        k = jnp.where(early, f // 2, n_hop - 1 - f // 2)
-        way = f % 2
-        mine = e < 2
-        slot = jnp.where(mine, own + e, way * n_hop + k)
-        half = jnp.where(mine, e, (k + way) % 2)
-        hop = k // 2 + 1
+        first, early = e < n_first, e < n_early
+        past = jnp.maximum(e - n_first, 0)
+        head = jnp.where(first, 0, 1 + lax.div(past, n_block))
+        b = lax.rem(past, n_block)
+        mine = jnp.where(first, e, b) < 2
+        f = jnp.maximum(jnp.where(early, e - 2, jnp.where(first, e - n_early, b - 2)), 0)
+        step = lax.div(f, 2)
+        way = f - 2 * step
+        k = jnp.where(early, step, n_hop - 1 - step)
+        half = jnp.where(mine, jnp.where(first, e, b), lax.rem(k + way, 2))
+        slot = jnp.where(mine, own + half, way * n_hop + k)
+        hop = lax.div(k, 2) + 1
         key_chip = jnp.where(mine, chip, lax.rem(chip + jnp.where(way == 1, hop, n_chip - hop), n_chip))
         pos0 = (key_chip * CORES + core) * keys_local + half * key_tile
-        s_lo = jnp.minimum(jnp.maximum(pos0 - sub_start - span * chip - span + sub_len, 0) // sub_len, n_sub - 1)
-        return slot, head, key_chip, half, s_lo // RUNS
-
-    counts, ends, n_taken = [], [], []
+        s_lo = jnp.minimum(lax.div(jnp.maximum(pos0 - sub_start - span * chip - span + sub_len, 0), sub_len * RUNS), n_run - 1)
+        return slot, head, key_chip, half, s_lo
+
+    taken, until, n_taken = [], [], jnp.int32(0)
     total = jnp.int32(0)
-    for head in range(n_kv):
-        base, taken = total, []
-        for e in range(n_block):
-            n = n_run - place(jnp.int32(e))[4]
-            if e < n_early:
-                fits = jnp.int32(1) if e < 2 else (total + n <= base + EARLY_ITEMS[min(head, 1)]).astype(jnp.int32)
-                taken.append(fits * taken[-1] if e > 2 else fits)
-                n = n * taken[-1]
-            else:
-                f = e - n_early
-                i_early = 2 + 2 * (n_hop - 1 - f // 2) + f % 2
-                if i_early < n_early:
-                    n = n * (1 - taken[i_early])
-            total = total + n
-            counts.append(n)
-            ends.append(total)
-        n_taken.append(sum(taken[1:], taken[0]))
+    for e in range(n_entry):
+        n = n_run - place(jnp.int32(e))[4]
+        if e < n_early:
+            fits = jnp.int32(1) if e < 2 else (total + n <= EARLY_ITEMS).astype(jnp.int32) * taken[-1]
+            taken.append(fits)
+            n_taken = n_taken + fits
+            n = n * fits
+        elif e < n_first:
+            f = e - n_early
+            i_early = 2 + 2 * (n_hop - 1 - f // 2) + f % 2
+            if i_early < n_early:
+                n = n * (1 - taken[i_early])
+        total = total + n
+        until.append(total)
 
     def following(at):
         i, e, j, n = at
         over = j + 1 >= n
-        head, b = e // n_block, lax.rem(e, n_block) + 1
-        limit = n_taken[0]
-        for h in range(1, n_kv):
-            limit = jnp.where(head == h, n_taken[h], limit)
-        b = jnp.where(b == limit, n_early, b)
-        f = b - n_early
-        gone = lambda f: (f >= 0) & (2 + 2 * (n_hop - 1 - f // 2) + f % 2 < limit)
-        b = jnp.where(gone(f), jnp.where((f % 2 == 1) | gone(f + 1), n_block, b + 1), b)
-        e1 = jnp.minimum(head * n_block + b, n_kv * n_block - 1)
+        e1 = e + 1
+        e1 = jnp.where(e1 == n_taken, n_early, e1)
+        f = e1 - n_early
+        back = n_hop - 1 - lax.div(jnp.maximum(f, 0), 2)
+        odd = lax.rem(jnp.maximum(f, 0), 2)
+        inside = (f >= 0) & (f < 2 * n_hop)
+        gone = inside & (2 + 2 * back + odd < n_taken)
+        both = (odd == 1) | (3 + 2 * back < n_taken)
+        e1 = jnp.where(gone, jnp.where(both, n_first, e1 + 1), e1)
+        e1 = jnp.minimum(e1, n_entry - 1)
         e, j = jnp.where(over, e1, e), jnp.where(over, 0, j + 1)
         slot, head, key_chip, half, s_lo = place(e)
         i = i + 1
@@ -253,12 +264,6 @@
 
         return i + m * UNROLL, lax.fori_loop(0, m, step, carry)
 
-    def end_of(e):
-        out = jnp.int32(0)
-        for v, n in enumerate(counts):
-            out = out + jnp.where(e >= v, n, 0)
-        return out
-
     def add(dst, src, head):
         cut = key_tile // 4
 
@@ -270,43 +275,71 @@
     def partial(i, head, peer):
         return remote(acc.at[i, head], rsb.at[i, head], rs_send.at[i, head], rs_recv.at[i, head], peer)
 
-    def send_sums(k, way, head, state=None):
-        i = way * n_hop + k
-        peer = jnp.where(way == 0, left, right)
-        if state is not None:
-            state = advance(state, end_of(head * n_block + n_early + 2 * (n_hop - 1 - k) + way) + UNROLL)
-
-        @pl.when(k + 2 < n_hop)
+    half_rows = lambda which: dqa.at[:, :, :, pl.ds(which * rows, rows)]
+    swap = remote(half_rows(1), dqr, x_send.at[3], x_recv.at[3], sibling)
+
+    GATHER, SUMS, WORK, OWN, ALL = 0, 1, 2, 3, 63
+    steps, arrived = [], [1, 0]
+    for word in ORDER.split():
+        kind, digits = word[0], word[1:]
+        head = 1 if kind in 'ET' else 0
+        if arrived[0] < n_hop:
+            bound = min(2 * arrived[0] + 1, n_early - 1)
+        else:
+            bound = n_entry - 1 if arrived[1] == n_hop else n_first + 1
+        k = way = items = 0
+        if kind in 'eE':
+            what, k = GATHER, int(digits)
+            arrived[head] = k + 1
+        elif kind in 'RT':
+            what, k, way = SUMS, int(digits[0]), int(digits[1])
+            bound = (n_first + 2 if head else n_early) + 2 * (n_hop - 1 - k) + way
+        elif kind == 'O':
+            what = OWN
+        else:
+            what, items = WORK, ALL if kind == 'F' else int(digits)
+        steps.append(what + 4 * (k + 16 * (way + 2 * (head + 2 * (items + 64 * bound)))))
+    def pick(table, t):
+        out = jnp.int32(0)
+        for j, x in enumerate(table):
+            out = out + jnp.where(t == j, x, 0)
+        return out
+
+    def carry_out(t, state):
+        number = pick(steps, t)
+        what, number = lax.rem(number, 4), lax.div(number, 4)
+        k, number = lax.rem(number, 16), lax.div(number, 16)
+        way, number = lax.rem(number, 2), lax.div(number, 2)
+        head, number = lax.rem(number, 2), lax.div(number, 2)
+        items, bound = lax.rem(number, 64), lax.div(number, 64)
+        last = pick(until, bound)
+        some = jnp.where(items == ALL, last + UNROLL, jnp.minimum(state[0] + items, last))
+        state = advance(state, jnp.where(what == SUMS, last + UNROLL, jnp.where(what == WORK, some, state[0])))
+
+        @pl.when(what == GATHER)
         def _():
-            partial(i + 2, head, peer).wait_recv()
-            add(i, i + 2, head)
-
-        partial(i, head, peer).start()
-        return state
-
-    def arrive(k, state):
-        goal = (EARLY_ITEMS[0] * k) // (n_hop - 1)
-        state = advance(state, jnp.minimum(goal, end_of(jnp.minimum(2 * k + 1, n_early - 1))))
-        pass_on(k, 0)
-
-        @pl.when(k == max(n_hop - 3, 1))
+            pass_on(k, head)
+
+        @pl.when(what == OWN)
         def _():
             gather_own(1)
+
+        @pl.when(items == ALL)
+        def _():
+            swap.start()
+
+        @pl.when(what == SUMS)
+        def _():
+            i = way * n_hop + k
+            peer = jnp.where(way == 0, left, right)
+
+            @pl.when(k + 2 < n_hop)
+            def _():
+                partial(i + 2, head, peer).wait_recv()
+                add(i, i + 2, head)
+
+            partial(i, head, peer).start()
         return state
-
-    def both(head):
-        def trip(m, state):
-            state = lax.fori_loop(0, 2, lambda way, state: send_sums(n_hop - 1 - m, way, head, state), state)
-            base = ends[(head + 1) * n_block - 1]
-            goal = jnp.minimum(base + (EARLY_ITEMS[1] * (m + 1)) // n_hop, end_of((head + 1) * n_block + jnp.minimum(2 * m + 1, n_early - 1)))
-            state = advance(state, jnp.where(state[0] >= base, goal, state[0]))
-            pass_on(m, head + 1)
-            if head + 2 < n_kv:
-                @pl.when(m == max(n_hop - 3, 1))
-                def _():
-                    gather_own(head + 2)
-            return state
-        return trip
 
     def settle(head):
         for k in (1, 0):
@@ -322,17 +355,7 @@
 
     zero = jnp.int32(0)
     start, at = following((zero - 1, zero, zero - 1, zero + 1))
-    state = (zero, (start[:3], start, at))
-    state = lax.fori_loop(1, n_hop, arrive, state)
-    for head in range(n_kv - 1):
-        state = lax.fori_loop(0, n_hop, both(head), state)
-    state = lax.fori_loop(0, 2 * n_hop - 2, lambda m, state: send_sums(n_hop - 1 - m // 2, m % 2, n_kv - 1, state), state)
-    state = advance(state, total + UNROLL)
-    half_rows = lambda which: dqa.at[:, :, :, pl.ds(which * rows, rows)]
-    swap = remote(half_rows(1), dqr, x_send.at[3], x_recv.at[3], sibling)
-    swap.start()
-    for way in range(2):
-        send_sums(0, way, n_kv - 1)
+    lax.fori_loop(0, len(steps), carry_out, (zero, (start[:3], start, at)))
     swap.wait_recv()
 
     @pl.loop(0, n_sub)

time: 170 us -> 169 us (level)
  no operation moved by 1% of the time
where the time goes in v9:
time: 169 us
  Pallas kernels  169 us (100%)
    pallas_call x1, Pallas kernels, local_backward(): pl.pallas_call(functools.partial(ring_kernel, cp_size, sub_start, scale),...  166 us

profile of v9, /device:TPU:22, one launch (start us, length us, event | category | flops | bytes accessed | tf_op | source)
XLA Modules:
  0.0 169.2 jit_solution(2796863132488154476)
XLA Ops:
  0.6 165.9 %ring_backward.1 = (bf16[16,32,2,4,128]{4,3,2,1,0:T(4,128)(2,1)}, f32[640,2,128]{2,1,0:T(2,128)}, f32[640,2,128]{2,1,0:T(2,128)}) custom-call(bf16[640,2,128]{2,1,0:T(2,128)(2,1)} %k_in.1, bf16[640,2,128]{2,1,0:T(2,128)(2,1)} %v_in.1, bf16[16,32,2,4,128]{4,3,2,1,0:T(4,128)(2,1)} %bitcast.6, bf16[16,32,2,4,128]{4,3,2,1,0:T(4,128)(2,1)} %bitcast.7, ...), custom_call_target="tpu_custom_call" | custom-call | flops 46976204800 | bytes 31457280 | tf_op jit(solution)/shard_map/ring_backward/pallas_call | solution.py:417
  166.5 2.7 %results.1 = (bf16[16,32,2,4,128]{4,3,2,1,0:T(4,128)(2,1)}, f32[640,2,128]{2,1,0:T(2,128)}, f32[640,2,128]{2,1,0:T(2,128)}) custom-call(bf16[16,32,2,4,128]{4,3,2,1,0:T(4,128)(2,1)} %get-tuple-element.9.a, f32[640,2,128]{2,1,0:T(2,128)} %get-tuple-element.10.b, f32[640,2,128]{2,1,0:T(2,128)} %get-tuple-element.11.c), custom_call_target="tpu_custom_call" | custom-call | bytes 4194304 | tf_op jit(solution)/shard_map/results/pallas_call | solution.py:451

commit v10 on v9

--- a/solution.py
+++ b/solution.py
@@ -15,7 +15,7 @@
 RUNS = 2
 UNROLL = 2
 EARLY_ITEMS = 26
-ORDER = ('e1 W4 e2 W4 e3 W4 e4 O W4 e5 W4 e6 R60 R61 E0 R50 R51 E1 R40 R41 E2 R30 R31 E3 R20 R21 E4 R10 R11 E5 R00 R01 E6 '
+ORDER = ('e1 W6 e2 e3 W6 e4 W4 O W8 e5 e6 W4 E0 R60 E1 R61 R50 E2 R51 R40 R41 W10 E3 W8 R30 R31 R20 R21 E4 E5 R10 R11 W4 R00 R01 W2 E6 '
          'T60 T61 T50 T51 T40 T41 T30 T31 T20 T21 T10 T11 F T00 T01')
 F32 = jnp.float32
 BF16 = jnp.bfloat16

time: 169 us -> 164 us (0.970)
  Pallas kernels: 169 us -> 163 us
    pallas_call x1, Pallas kernels: 166 us -> 160 us  [local_backward(): pl.pallas_call(functools.partial(ring_kernel, cp_size, sub_start, scale),...]
where the time goes in v10:
time: 164 us; the launch traced here: 163 us
  Pallas kernels  163 us (99%)
    pallas_call x1, Pallas kernels, local_backward(): pl.pallas_call(functools.partial(ring_kernel, cp_size, sub_start, scale),...  160 us

profile of v10, /device:TPU:22, one launch (start us, length us, event | category | flops | bytes accessed | tf_op | source)
XLA Modules:
  0.0 163.5 jit_solution(11618706344691112983)
XLA Ops:
  0.6 160.2 %ring_backward.1 = (bf16[16,32,2,4,128]{4,3,2,1,0:T(4,128)(2,1)}, f32[640,2,128]{2,1,0:T(2,128)}, f32[640,2,128]{2,1,0:T(2,128)}) custom-call(bf16[640,2,128]{2,1,0:T(2,128)(2,1)} %k_in.1, bf16[640,2,128]{2,1,0:T(2,128)(2,1)} %v_in.1, bf16[16,32,2,4,128]{4,3,2,1,0:T(4,128)(2,1)} %bitcast.6, bf16[16,32,2,4,128]{4,3,2,1,0:T(4,128)(2,1)} %bitcast.7, ...), custom_call_target="tpu_custom_call" | custom-call | flops 46976204800 | bytes 31457280 | tf_op jit(solution)/shard_map/ring_backward/pallas_call | solution.py:417
  160.8 2.7 %results.1 = (bf16[16,32,2,4,128]{4,3,2,1,0:T(4,128)(2,1)}, f32[640,2,128]{2,1,0:T(2,128)}, f32[640,2,128]{2,1,0:T(2,128)}) custom-call(bf16[16,32,2,4,128]{4,3,2,1,0:T(4,128)(2,1)} %get-tuple-element.9.a, f32[640,2,128]{2,1,0:T(2,128)} %get-tuple-element.10.b, f32[640,2,128]{2,1,0:T(2,128)} %get-tuple-element.11.c), custom_call_target="tpu_custom_call" | custom-call | bytes 4194304 | tf_op jit(solution)/shard_map/results/pallas_call | solution.py:451

commit v11 on v10

--- a/solution.py
+++ b/solution.py
@@ -12,6 +12,7 @@
 CORES = 2
 LANES = 128
 SPLIT = 64
+PIECES = 4
 RUNS = 2
 UNROLL = 2
 EARLY_ITEMS = 26
@@ -59,15 +60,17 @@
 
     for c in own_kv:
         c.wait()
-    for half in range(2):
+
+    def split(h):
         @pl.loop(0, key_tile // SPLIT)
         def _(i):
             r = pl.multiple_of(i * SPLIT, SPLIT)
-            for part in range(2):
-                x = raw_kv[part, pl.ds(half * key_tile + r, SPLIT)].astype(F32)
-                for h in range(n_kv):
+            for half in range(2):
+                for part in range(2):
+                    x = raw_kv[part, pl.ds(half * key_tile + r, SPLIT)].astype(F32)
                     kvb[own + half, h, pl.ds(r, SPLIT), part * head_dim:(part + 1) * head_dim] = x[:, h].astype(BF16)
 
+    split(0)
     pl.semaphore_wait(barrier, 3)
 
     def remote(src, dst, send, recv, peer):
@@ -76,7 +79,7 @@
 
     def gather(way, k, head, src=None):
         i = way * n_hop + k
-        return remote(kvb.at[i, head] if src is None else src, kvb.at[i, head], ag_send.at[i, head], ag_recv.at[i, head], nbr[way])
+        return remote(kvb.at[i, head] if src is None else src, kvb.at[i, head], ag_send.at[0], ag_recv.at[i, head], nbr[way])
 
     def gather_own(head):
         for j in range(2):
@@ -93,6 +96,8 @@
                 gather(way, k + 2, head, kvb.at[i, head]).start()
 
     gather_own(0)
+    for h in range(1, n_kv):
+        split(h)
     share = [remote(q_in, raw_q.at[1], x_send.at[0], x_recv.at[0], sibling),
              remote(do_in, raw_do.at[1], x_send.at[1], x_recv.at[1], sibling)]
     for c in share:
@@ -273,7 +278,7 @@
             acc[dst, head, r, :] += rsb[src, head, r, :]
 
     def partial(i, head, peer):
-        return remote(acc.at[i, head], rsb.at[i, head], rs_send.at[i, head], rs_recv.at[i, head], peer)
+        return remote(acc.at[i, head], rsb.at[i, head], rs_send.at[0], rs_recv.at[i, head], peer)
 
     half_rows = lambda which: dqa.at[:, :, :, pl.ds(which * rows, rows)]
     swap = remote(half_rows(1), dqr, x_send.at[3], x_recv.at[3], sibling)
@@ -341,17 +346,14 @@
             partial(i, head, peer).start()
         return state
 
-    def settle(head):
+    def settle(head, half):
         for k in (1, 0):
-            for way in range(2):
-                partial(way * n_hop + k, head, nbr[1 - way]).wait_recv()
-                add(own + (k + way) % 2, way * n_hop + k, head)
-
-        @pl.loop(0, 2)
-        def _(half):
-            r = pl.ds(pl.multiple_of(half * key_tile, 8), key_tile)
-            dko[r, head, :] = acc[own + half, head, :, :head_dim] * scale
-            dvo[r, head, :] = acc[own + half, head, :, head_dim:]
+            way = (half + k) % 2
+            partial(way * n_hop + k, head, nbr[1 - way]).wait_recv()
+            add(own + half, way * n_hop + k, head)
+        r = slice(half * key_tile, (half + 1) * key_tile)
+        dko[r, head, :] = acc[own + half, head, :, :head_dim] * scale
+        dvo[r, head, :] = acc[own + half, head, :, head_dim:]
 
     zero = jnp.int32(0)
     start, at = following((zero - 1, zero, zero - 1, zero + 1))
@@ -364,31 +366,40 @@
             x = ((dqa[h, s, :, :rows] + dqr[h, s]) * scale).astype(BF16).T
             raw_q[0, s, :, h] = x.reshape(local_len, group, head_dim)
 
-    puts = [pltpu.make_async_copy(a, b, out_sem.at[i]) for i, (a, b) in enumerate(((raw_q.at[0], dq_out), (dko, dk_out), (dvo, dv_out)))]
+    puts = [pltpu.make_async_copy(raw_q.at[0], dq_out, out_sem.at[0])]
     puts[0].start()
-    for head in range(n_kv):
-        settle(head)
-    puts[1].start()
-    puts[2].start()
+    for head in range(n_kv - 1):
+        for half in range(2):
+            settle(head, half)
+    for half in range(2):
+        settle(n_kv - 1, half)
+        r = pl.ds(half * key_tile, key_tile)
+        for i, (a, b) in enumerate(((dko, dk_out), (dvo, dv_out))):
+            c = pltpu.make_async_copy(a.at[r], b.at[r], out_sem.at[1 + 2 * half + i])
+            c.start()
+            puts.append(c)
     swap.wait_send()
-    for way in range(2):
-        for k in range(n_hop):
-            for head in range(n_kv):
-                gather(way, k, head).wait_send()
-                partial(way * n_hop + k, head, nbr[1 - way]).wait_send()
+    moved = pl.ds(0, 2 * n_hop)
+    remote(kvb.at[moved], kvb.at[moved], ag_send.at[0], ag_recv.at[0, 0], right).wait_send()
+    remote(acc.at[moved], rsb.at[moved], rs_send.at[0], rs_recv.at[0, 0], right).wait_send()
     for c in puts:
         c.wait()
 
 
 def copy_kernel(a, b, c, a_out, b_out, c_out, a_buf, b_buf, c_buf, in_sem, out_sem):
-    ins = [pltpu.make_async_copy(x, y, in_sem.at[i]) for i, (x, y) in enumerate(((a, a_buf), (b, b_buf), (c, c_buf)))]
-    outs = [pltpu.make_async_copy(x, y, out_sem.at[i]) for i, (x, y) in enumerate(((a_buf, a_out), (b_buf, b_out), (c_buf, c_out)))]
-    for x in ins:
+    moves = []
+    for src, buf, dst in ((a, a_buf, a_out), (b, b_buf, b_out), (c, c_buf, c_out)):
+        piece = src.shape[0] // PIECES
+        for i in range(PIECES):
+            r, n = pl.ds(i * piece, piece), len(moves)
+            moves.append((pltpu.make_async_copy(src.at[r], buf.at[r], in_sem.at[n]),
+                          pltpu.make_async_copy(buf.at[r], dst.at[r], out_sem.at[n])))
+    for x, _ in moves:
         x.start()
-    for x, y in zip(ins, outs):
+    for x, y in moves:
         x.wait()
         y.start()
-    for y in outs:
+    for _, y in moves:
         y.wait()
 
 
@@ -442,8 +453,8 @@
                 vmem((2, half, RUNS * CORES * rows), BF16),
                 vmem((2, half, RUNS * CORES * rows), BF16),
                 vmem((2,) + key_act.shape, BF16),
-                dma((2 * n_hop, n_kv)), dma((2 * n_hop, n_kv)), dma((2 * n_hop, n_kv)), dma((2 * n_hop, n_kv)),
-                dma((4,)), dma((4,)), dma((7,)), dma((3,)),
+                dma((1,)), dma((2 * n_hop, n_kv)), dma((1,)), dma((2 * n_hop, n_kv)),
+                dma((4,)), dma((4,)), dma((7,)), dma((5,)),
             ],
             compiler_params=pltpu.CompilerParams(collective_id=0, has_side_effects=True, vmem_limit_bytes=62 * 1024 * 1024),
             cost_estimate=pl.CostEstimate(flops=flops, bytes_accessed=30 * 2 ** 20, transcendentals=0),
@@ -454,7 +465,7 @@
             out_shape=tuple(jax.ShapeDtypeStruct(x.shape, x.dtype) for x in (dq, dk, dv)),
             in_specs=[hbm] * 3,
             out_specs=(hbm,) * 3,
-            scratch_shapes=[vmem(x.shape, x.dtype) for x in (dq, dk, dv)] + [dma((3,)), dma((3,))],
+            scratch_shapes=[vmem(x.shape, x.dtype) for x in (dq, dk, dv)] + [dma((3 * PIECES,)), dma((3 * PIECES,))],
             cost_estimate=pl.CostEstimate(flops=0, bytes_accessed=2 ** 22, transcendentals=0),
         )(dq, dk, dv)
         return dq.reshape(query.shape), dk, dv

time: 164 us -> 162 us (0.988)
  no operation moved by 1% of the time
where the time goes in v11:
time: 162 us
  Pallas kernels  162 us (100%)
    pallas_call x1, Pallas kernels, local_backward(): pl.pallas_call(functools.partial(ring_kernel, cp_size, sub_start, scale),...  159 us

profile of v11, /device:TPU:22, one launch (start us, length us, event | category | flops | bytes accessed | tf_op | source)
XLA Modules:
  0.0 162.2 jit_solution(11428717526111715980)
XLA Ops:
  0.6 159.0 %ring_backward.1 = (bf16[16,32,2,4,128]{4,3,2,1,0:T(4,128)(2,1)}, f32[640,2,128]{2,1,0:T(2,128)}, f32[640,2,128]{2,1,0:T(2,128)}) custom-call(bf16[640,2,128]{2,1,0:T(2,128)(2,1)} %k_in.1, bf16[640,2,128]{2,1,0:T(2,128)(2,1)} %v_in.1, bf16[16,32,2,4,128]{4,3,2,1,0:T(4,128)(2,1)} %bitcast.6, bf16[16,32,2,4,128]{4,3,2,1,0:T(4,128)(2,1)} %bitcast.7, ...), custom_call_target="tpu_custom_call" | custom-call | flops 46976204800 | bytes 31457280 | tf_op jit(solution)/shard_map/ring_backward/pallas_call | solution.py:428
  159.6 2.5 %results.1 = (bf16[16,32,2,4,128]{4,3,2,1,0:T(4,128)(2,1)}, f32[640,2,128]{2,1,0:T(2,128)}, f32[640,2,128]{2,1,0:T(2,128)}) custom-call(bf16[16,32,2,4,128]{4,3,2,1,0:T(4,128)(2,1)} %get-tuple-element.9.a, f32[640,2,128]{2,1,0:T(2,128)} %get-tuple-element.10.b, f32[640,2,128]{2,1,0:T(2,128)} %get-tuple-element.11.c), custom_call_target="tpu_custom_call" | custom-call | bytes 4194304 | tf_op jit(solution)/shard_map/results/pallas_call | solution.py:462

commit v12 on v11

--- a/solution.py
+++ b/solution.py
@@ -50,7 +50,7 @@
     own_kv = [pltpu.make_async_copy(x, raw_kv.at[i], loc_sem.at[5 + i]) for i, x in enumerate((k_in, v_in))]
     local = [pltpu.make_async_copy(a, b, loc_sem.at[i]) for i, (a, b) in enumerate((
         (doc_in, docs), (lse_in, lse), (do_in, raw_do.at[0]), (o_in, raw_o), (q_in, raw_q.at[0])))]
-    for c in own_kv + local:
+    for c in own_kv:
         c.start()
 
     @pl.loop(0, n_sub)
@@ -96,12 +96,12 @@
                 gather(way, k + 2, head, kvb.at[i, head]).start()
 
     gather_own(0)
+    share = [remote(q_in, raw_q.at[1], x_send.at[0], x_recv.at[0], sibling),
+             remote(do_in, raw_do.at[1], x_send.at[1], x_recv.at[1], sibling)]
+    for c in local + share:
+        c.start()
     for h in range(1, n_kv):
         split(h)
-    share = [remote(q_in, raw_q.at[1], x_send.at[0], x_recv.at[0], sibling),
-             remote(do_in, raw_do.at[1], x_send.at[1], x_recv.at[1], sibling)]
-    for c in share:
-        c.start()
 
     def mine(which):
         return lines.at[:, :, :, pl.ds(which * rows, rows)]

time: 162 us -> 162 us (level)
  no operation moved by 1% of the time
where the time goes in v12:
time: 162 us
  Pallas kernels  162 us (100%)
    pallas_call x1, Pallas kernels, local_backward(): pl.pallas_call(functools.partial(ring_kernel, cp_size, sub_start, scale),...  159 us

profile of v12, /device:TPU:22, one launch (start us, length us, event | category | flops | bytes accessed | tf_op | source)
XLA Modules:
  0.0 162.2 jit_solution(9211738864034686187)
XLA Ops:
  0.6 159.0 %ring_backward.1 = (bf16[16,32,2,4,128]{4,3,2,1,0:T(4,128)(2,1)}, f32[640,2,128]{2,1,0:T(2,128)}, f32[640,2,128]{2,1,0:T(2,128)}) custom-call(bf16[640,2,128]{2,1,0:T(2,128)(2,1)} %k_in.1, bf16[640,2,128]{2,1,0:T(2,128)(2,1)} %v_in.1, bf16[16,32,2,4,128]{4,3,2,1,0:T(4,128)(2,1)} %bitcast.6, bf16[16,32,2,4,128]{4,3,2,1,0:T(4,128)(2,1)} %bitcast.7, ...), custom_call_target="tpu_custom_call" | custom-call | flops 46976204800 | bytes 31457280 | tf_op jit(solution)/shard_map/ring_backward/pallas_call | solution.py:428
  159.6 2.5 %results.1 = (bf16[16,32,2,4,128]{4,3,2,1,0:T(4,128)(2,1)}, f32[640,2,128]{2,1,0:T(2,128)}, f32[640,2,128]{2,1,0:T(2,128)}) custom-call(bf16[16,32,2,4,128]{4,3,2,1,0:T(4,128)(2,1)} %get-tuple-element.9.a, f32[640,2,128]{2,1,0:T(2,128)} %get-tuple-element.10.b, f32[640,2,128]{2,1,0:T(2,128)} %get-tuple-element.11.c), custom_call_target="tpu_custom_call" | custom-call | bytes 4194304 | tf_op jit(solution)/shard_map/results/pallas_call | solution.py:462

commit v13 on v12

--- a/solution.py
+++ b/solution.py
@@ -12,7 +12,7 @@
 CORES = 2
 LANES = 128
 SPLIT = 64
-PIECES = 4
+PIECES = 8
 RUNS = 2
 UNROLL = 2
 EARLY_ITEMS = 26
@@ -47,10 +47,12 @@
     for peer in (right, left, sibling):
         pl.semaphore_signal(barrier, inc=1, device_id={'cp': peer}, device_id_type=MESH)
 
-    own_kv = [pltpu.make_async_copy(x, raw_kv.at[i], loc_sem.at[5 + i]) for i, x in enumerate((k_in, v_in))]
+    halves = [pl.ds(half * key_tile, key_tile) for half in range(2)]
+    own_kv = [[pltpu.make_async_copy(x.at[r], raw_kv.at[i, r], loc_sem.at[5 + 2 * half + i]) for i, x in enumerate((k_in, v_in))]
+              for half, r in enumerate(halves)]
     local = [pltpu.make_async_copy(a, b, loc_sem.at[i]) for i, (a, b) in enumerate((
         (doc_in, docs), (lse_in, lse), (do_in, raw_do.at[0]), (o_in, raw_o), (q_in, raw_q.at[0])))]
-    for c in own_kv:
+    for c in own_kv[0] + own_kv[1]:
         c.start()
 
     @pl.loop(0, n_sub)
@@ -58,19 +60,18 @@
         for h in range(n_kv):
             dqa[h, s] = jnp.zeros(dqa.shape[2:], F32)
 
-    for c in own_kv:
-        c.wait()
-
-    def split(h):
+    def split(h, half):
         @pl.loop(0, key_tile // SPLIT)
         def _(i):
             r = pl.multiple_of(i * SPLIT, SPLIT)
-            for half in range(2):
-                for part in range(2):
-                    x = raw_kv[part, pl.ds(half * key_tile + r, SPLIT)].astype(F32)
-                    kvb[own + half, h, pl.ds(r, SPLIT), part * head_dim:(part + 1) * head_dim] = x[:, h].astype(BF16)
-
-    split(0)
+            for part in range(2):
+                x = raw_kv[part, pl.ds(half * key_tile + r, SPLIT)].astype(F32)
+                kvb[own + half, h, pl.ds(r, SPLIT), part * head_dim:(part + 1) * head_dim] = x[:, h].astype(BF16)
+
+    for half in range(2):
+        for c in own_kv[half]:
+            c.wait()
+        split(0, half)
     pl.semaphore_wait(barrier, 3)
 
     def remote(src, dst, send, recv, peer):
@@ -101,7 +102,8 @@
     for c in local + share:
         c.start()
     for h in range(1, n_kv):
-        split(h)
+        for half in range(2):
+            split(h, half)
 
     def mine(which):
         return lines.at[:, :, :, pl.ds(which * rows, rows)]
@@ -454,7 +456,7 @@
                 vmem((2, half, RUNS * CORES * rows), BF16),
                 vmem((2,) + key_act.shape, BF16),
                 dma((1,)), dma((2 * n_hop, n_kv)), dma((1,)), dma((2 * n_hop, n_kv)),
-                dma((4,)), dma((4,)), dma((7,)), dma((5,)),
+                dma((4,)), dma((4,)), dma((9,)), dma((5,)),
             ],
             compiler_params=pltpu.CompilerParams(collective_id=0, has_side_effects=True, vmem_limit_bytes=62 * 1024 * 1024),
             cost_estimate=pl.CostEstimate(flops=flops, bytes_accessed=30 * 2 ** 20, transcendentals=0),

time: 162 us -> 163 us (level)
  no operation moved by 1% of the time
where the time goes in v13:
time: 163 us; the launch traced here: 162 us
  Pallas kernels  162 us (99%)
    pallas_call x1, Pallas kernels, local_backward(): pl.pallas_call(functools.partial(ring_kernel, cp_size, sub_start, scale),...  159 us

profile of v13, /device:TPU:22, one launch (start us, length us, event | category | flops | bytes accessed | tf_op | source)
XLA Modules:
  0.0 162.4 jit_solution(14234078718284866383)
XLA Ops:
  0.6 158.9 %ring_backward.1 = (bf16[16,32,2,4,128]{4,3,2,1,0:T(4,128)(2,1)}, f32[640,2,128]{2,1,0:T(2,128)}, f32[640,2,128]{2,1,0:T(2,128)}) custom-call(bf16[640,2,128]{2,1,0:T(2,128)(2,1)} %k_in.1, bf16[640,2,128]{2,1,0:T(2,128)(2,1)} %v_in.1, bf16[16,32,2,4,128]{4,3,2,1,0:T(4,128)(2,1)} %bitcast.6, bf16[16,32,2,4,128]{4,3,2,1,0:T(4,128)(2,1)} %bitcast.7, ...), custom_call_target="tpu_custom_call" | custom-call | flops 46976204800 | bytes 31457280 | tf_op jit(solution)/shard_map/ring_backward/pallas_call | solution.py:430
  159.6 2.8 %results.1 = (bf16[16,32,2,4,128]{4,3,2,1,0:T(4,128)(2,1)}, f32[640,2,128]{2,1,0:T(2,128)}, f32[640,2,128]{2,1,0:T(2,128)}) custom-call(bf16[16,32,2,4,128]{4,3,2,1,0:T(4,128)(2,1)} %get-tuple-element.9.a, f32[640,2,128]{2,1,0:T(2,128)} %get-tuple-element.10.b, f32[640,2,128]{2,1,0:T(2,128)} %get-tuple-element.11.c), custom_call_target="tpu_custom_call" | custom-call | bytes 4194304 | tf_op jit(solution)/shard_map/results/pallas_call | solution.py:464

commit v14 on v12

--- a/solution.py
+++ b/solution.py
@@ -394,11 +394,11 @@
             r, n = pl.ds(i * piece, piece), len(moves)
             moves.append((pltpu.make_async_copy(src.at[r], buf.at[r], in_sem.at[n]),
                           pltpu.make_async_copy(buf.at[r], dst.at[r], out_sem.at[n])))
-    for x, _ in moves:
-        x.start()
-    for x, y in moves:
+    for n, (x, _) in enumerate(moves):
+        x.start(priority=n % 2)
+    for n, (x, y) in enumerate(moves):
         x.wait()
-        y.start()
+        y.start(priority=n % 2)
     for _, y in moves:
         y.wait()
 

time: 162 us -> 163 us (level)
  no operation moved by 1% of the time
where the time goes in v14:
time: 163 us; the launch traced here: 162 us
  Pallas kernels  162 us (99%)
    pallas_call x1, Pallas kernels, local_backward(): pl.pallas_call(functools.partial(ring_kernel, cp_size, sub_start, scale),...  159 us

profile of v14, /device:TPU:22, one launch (start us, length us, event | category | flops | bytes accessed | tf_op | source)
XLA Modules:
  0.0 162.4 jit_solution(14664545964856117867)
XLA Ops:
  0.6 159.0 %ring_backward.1 = (bf16[16,32,2,4,128]{4,3,2,1,0:T(4,128)(2,1)}, f32[640,2,128]{2,1,0:T(2,128)}, f32[640,2,128]{2,1,0:T(2,128)}) custom-call(bf16[640,2,128]{2,1,0:T(2,128)(2,1)} %k_in.1, bf16[640,2,128]{2,1,0:T(2,128)(2,1)} %v_in.1, bf16[16,32,2,4,128]{4,3,2,1,0:T(4,128)(2,1)} %bitcast.6, bf16[16,32,2,4,128]{4,3,2,1,0:T(4,128)(2,1)} %bitcast.7, ...), custom_call_target="tpu_custom_call" | custom-call | flops 46976204800 | bytes 31457280 | tf_op jit(solution)/shard_map/ring_backward/pallas_call | solution.py:428
  159.6 2.8 %results.1 = (bf16[16,32,2,4,128]{4,3,2,1,0:T(4,128)(2,1)}, f32[640,2,128]{2,1,0:T(2,128)}, f32[640,2,128]{2,1,0:T(2,128)}) custom-call(bf16[16,32,2,4,128]{4,3,2,1,0:T(4,128)(2,1)} %get-tuple-element.9.a, f32[640,2,128]{2,1,0:T(2,128)} %get-tuple-element.10.b, f32[640,2,128]{2,1,0:T(2,128)} %get-tuple-element.11.c), custom_call_target="tpu_custom_call" | custom-call | bytes 4194304 | tf_op jit(solution)/shard_map/results/pallas_call | solution.py:462

commit v15 on v11

--- a/solution.py
+++ b/solution.py
@@ -79,7 +79,7 @@
 
     def gather(way, k, head, src=None):
         i = way * n_hop + k
-        return remote(kvb.at[i, head] if src is None else src, kvb.at[i, head], ag_send.at[0], ag_recv.at[i, head], nbr[way])
+        return remote(kvb.at[i, head] if src is None else src, kvb.at[i, head], ag_send.at[0], ag_recv.at[k, head], nbr[way])
 
     def gather_own(head):
         for j in range(2):
@@ -87,8 +87,9 @@
                 gather(way, j, head, kvb.at[own + (j + way) % 2, head]).start()
 
     def pass_on(k, head):
+        two = kvb.at[pl.ds(0, 2), head]
+        remote(two, two, ag_send.at[0], ag_recv.at[k, head], right).wait_recv()
         for way in range(2):
-            gather(way, k, head).wait_recv()
             i = way * n_hop + k
 
             @pl.when(k + 2 < n_hop)
@@ -277,8 +278,10 @@
             r = pl.ds(pl.multiple_of(i * cut, 8), cut)
             acc[dst, head, r, :] += rsb[src, head, r, :]
 
-    def partial(i, head, peer):
-        return remote(acc.at[i, head], rsb.at[i, head], rs_send.at[0], rs_recv.at[i, head], peer)
+    def partial(way, k, head, peer):
+        i = way * n_hop + k
+        sem = rs_recv.at[jnp.where(k < 2, way * n_hop + k, k), head]
+        return remote(acc.at[i, head], rsb.at[i, head], rs_send.at[0], sem, peer)
 
     half_rows = lambda which: dqa.at[:, :, :, pl.ds(which * rows, rows)]
     swap = remote(half_rows(1), dqr, x_send.at[3], x_recv.at[3], sibling)
@@ -338,18 +341,22 @@
             i = way * n_hop + k
             peer = jnp.where(way == 0, left, right)
 
+            @pl.when((k + 2 < n_hop) & (way == 0))
+            def _():
+                two = pl.ds(0, 2)
+                remote(acc.at[two, head], rsb.at[two, head], rs_send.at[0], rs_recv.at[k + 2, head], peer).wait_recv()
+
             @pl.when(k + 2 < n_hop)
             def _():
-                partial(i + 2, head, peer).wait_recv()
                 add(i, i + 2, head)
 
-            partial(i, head, peer).start()
+            partial(way, k, head, peer).start()
         return state
 
     def settle(head, half):
         for k in (1, 0):
             way = (half + k) % 2
-            partial(way * n_hop + k, head, nbr[1 - way]).wait_recv()
+            partial(way, k, head, nbr[1 - way]).wait_recv()
             add(own + half, way * n_hop + k, head)
         r = slice(half * key_tile, (half + 1) * key_tile)
         dko[r, head, :] = acc[own + half, head, :, :head_dim] * scale
@@ -453,7 +460,7 @@
                 vmem((2, half, RUNS * CORES * rows), BF16),
                 vmem((2, half, RUNS * CORES * rows), BF16),
                 vmem((2,) + key_act.shape, BF16),
-                dma((1,)), dma((2 * n_hop, n_kv)), dma((1,)), dma((2 * n_hop, n_kv)),
+                dma((1,)), dma((n_hop, n_kv)), dma((1,)), dma((n_hop + 2, n_kv)),
                 dma((4,)), dma((4,)), dma((7,)), dma((5,)),
             ],
             compiler_params=pltpu.CompilerParams(collective_id=0, has_side_effects=True, vmem_limit_bytes=62 * 1024 * 1024),

time: 162 us -> 162 us (level)
  no operation moved by 1% of the time
where the time goes in v15:
time: 162 us
  Pallas kernels  161 us (99%)
    pallas_call x1, Pallas kernels, local_backward(): pl.pallas_call(functools.partial(ring_kernel, cp_size, sub_start, scale),...  159 us

profile of v15, /device:TPU:22, one launch (start us, length us, event | category | flops | bytes accessed | tf_op | source)
XLA Modules:
  0.0 161.9 jit_solution(2752769788068091866)
XLA Ops:
  0.6 158.7 %ring_backward.1 = (bf16[16,32,2,4,128]{4,3,2,1,0:T(4,128)(2,1)}, f32[640,2,128]{2,1,0:T(2,128)}, f32[640,2,128]{2,1,0:T(2,128)}) custom-call(bf16[640,2,128]{2,1,0:T(2,128)(2,1)} %k_in.1, bf16[640,2,128]{2,1,0:T(2,128)(2,1)} %v_in.1, bf16[16,32,2,4,128]{4,3,2,1,0:T(4,128)(2,1)} %bitcast.6, bf16[16,32,2,4,128]{4,3,2,1,0:T(4,128)(2,1)} %bitcast.7, ...), custom_call_target="tpu_custom_call" | custom-call | flops 46976204800 | bytes 31457280 | tf_op jit(solution)/shard_map/ring_backward/pallas_call | solution.py:435
  159.4 2.5 %results.1 = (bf16[16,32,2,4,128]{4,3,2,1,0:T(4,128)(2,1)}, f32[640,2,128]{2,1,0:T(2,128)}, f32[640,2,128]{2,1,0:T(2,128)}) custom-call(bf16[16,32,2,4,128]{4,3,2,1,0:T(4,128)(2,1)} %get-tuple-element.9.a, f32[640,2,128]{2,1,0:T(2,128)} %get-tuple-element.10.b, f32[640,2,128]{2,1,0:T(2,128)} %get-tuple-element.11.c), custom_call_target="tpu_custom_call" | custom-call | bytes 4194304 | tf_op jit(solution)/shard_map/results/pallas_call | solution.py:469

commit v16 on v15

--- a/solution.py
+++ b/solution.py
@@ -354,13 +354,13 @@
         return state
 
     def settle(head, half):
-        for k in (1, 0):
-            way = (half + k) % 2
-            partial(way, k, head, nbr[1 - way]).wait_recv()
-            add(own + half, way * n_hop + k, head)
+        near, far = half * n_hop, (1 - half) * n_hop + 1
+        partial(1 - half, 1, head, nbr[half]).wait_recv()
+        add(own + half, far, head)
+        partial(half, 0, head, nbr[1 - half]).wait_recv()
         r = slice(half * key_tile, (half + 1) * key_tile)
-        dko[r, head, :] = acc[own + half, head, :, :head_dim] * scale
-        dvo[r, head, :] = acc[own + half, head, :, head_dim:]
+        dko[r, head, :] = (acc[own + half, head, :, :head_dim] + rsb[near, head, :, :head_dim]) * scale
+        dvo[r, head, :] = acc[own + half, head, :, head_dim:] + rsb[near, head, :, head_dim:]
 
     zero = jnp.int32(0)
     start, at = following((zero - 1, zero, zero - 1, zero + 1))

time: 162 us -> 162 us (level)
  no operation moved by 1% of the time
where the time goes in v16:
time: 162 us
  Pallas kernels  161 us (99%)
    pallas_call x1, Pallas kernels, local_backward(): pl.pallas_call(functools.partial(ring_kernel, cp_size, sub_start, scale),...  159 us

profile of v16, /device:TPU:22, one launch (start us, length us, event | category | flops | bytes accessed | tf_op | source)
XLA Modules:
  0.0 161.9 jit_solution(8556041668837012293)
XLA Ops:
  0.6 158.7 %ring_backward.1 = (bf16[16,32,2,4,128]{4,3,2,1,0:T(4,128)(2,1)}, f32[640,2,128]{2,1,0:T(2,128)}, f32[640,2,128]{2,1,0:T(2,128)}) custom-call(bf16[640,2,128]{2,1,0:T(2,128)(2,1)} %k_in.1, bf16[640,2,128]{2,1,0:T(2,128)(2,1)} %v_in.1, bf16[16,32,2,4,128]{4,3,2,1,0:T(4,128)(2,1)} %bitcast.6, bf16[16,32,2,4,128]{4,3,2,1,0:T(4,128)(2,1)} %bitcast.7, ...), custom_call_target="tpu_custom_call" | custom-call | flops 46976204800 | bytes 31457280 | tf_op jit(solution)/shard_map/ring_backward/pallas_call | solution.py:435
  159.4 2.5 %results.1 = (bf16[16,32,2,4,128]{4,3,2,1,0:T(4,128)(2,1)}, f32[640,2,128]{2,1,0:T(2,128)}, f32[640,2,128]{2,1,0:T(2,128)}) custom-call(bf16[16,32,2,4,128]{4,3,2,1,0:T(4,128)(2,1)} %get-tuple-element.9.a, f32[640,2,128]{2,1,0:T(2,128)} %get-tuple-element.10.b, f32[640,2,128]{2,1,0:T(2,128)} %get-tuple-element.11.c), custom_call_target="tpu_custom_call" | custom-call | bytes 4194304 | tf_op jit(solution)/shard_map/results/pallas_call | solution.py:469

commit v17 on v16

--- a/solution.py
+++ b/solution.py
@@ -12,7 +12,7 @@
 CORES = 2
 LANES = 128
 SPLIT = 64
-PIECES = 4
+PIECES = 2
 RUNS = 2
 UNROLL = 2
 EARLY_ITEMS = 26

time: 162 us -> 162 us (level)
  no operation moved by 1% of the time
where the time goes in v17:
time: 162 us
  Pallas kernels  161 us (99%)
    pallas_call x1, Pallas kernels, local_backward(): pl.pallas_call(functools.partial(ring_kernel, cp_size, sub_start, scale),...  159 us

profile of v17, /device:TPU:22, one launch (start us, length us, event | category | flops | bytes accessed | tf_op | source)
XLA Modules:
  0.0 161.9 jit_solution(15187036585945515706)
XLA Ops:
  0.6 158.7 %ring_backward.1 = (bf16[16,32,2,4,128]{4,3,2,1,0:T(4,128)(2,1)}, f32[640,2,128]{2,1,0:T(2,128)}, f32[640,2,128]{2,1,0:T(2,128)}) custom-call(bf16[640,2,128]{2,1,0:T(2,128)(2,1)} %k_in.1, bf16[640,2,128]{2,1,0:T(2,128)(2,1)} %v_in.1, bf16[16,32,2,4,128]{4,3,2,1,0:T(4,128)(2,1)} %bitcast.6, bf16[16,32,2,4,128]{4,3,2,1,0:T(4,128)(2,1)} %bitcast.7, ...), custom_call_target="tpu_custom_call" | custom-call | flops 46976204800 | bytes 31457280 | tf_op jit(solution)/shard_map/ring_backward/pallas_call | solution.py:435
  159.4 2.5 %results.1 = (bf16[16,32,2,4,128]{4,3,2,1,0:T(4,128)(2,1)}, f32[640,2,128]{2,1,0:T(2,128)}, f32[640,2,128]{2,1,0:T(2,128)}) custom-call(bf16[16,32,2,4,128]{4,3,2,1,0:T(4,128)(2,1)} %get-tuple-element.9.a, f32[640,2,128]{2,1,0:T(2,128)} %get-tuple-element.10.b, f32[640,2,128]{2,1,0:T(2,128)} %get-tuple-element.11.c), custom_call_target="tpu_custom_call" | custom-call | bytes 4194304 | tf_op jit(solution)/shard_map/results/pallas_call | solution.py:469

commit v18 on v17

--- a/solution.py
+++ b/solution.py
@@ -16,8 +16,11 @@
 RUNS = 2
 UNROLL = 2
 EARLY_ITEMS = 26
-ORDER = ('e1 W6 e2 e3 W6 e4 W4 O W8 e5 e6 W4 E0 R60 E1 R61 R50 E2 R51 R40 R41 W10 E3 W8 R30 R31 R20 R21 E4 E5 R10 R11 W4 R00 R01 W2 E6 '
-         'T60 T61 T50 T51 T40 T41 T30 T31 T20 T21 T10 T11 F T00 T01')
+ORDER = (
+    'e1', 'W6', 'e2', 'e3', 'W6', 'e4', 'W4', 'O', 'W8', 'e5', 'e6', 'W4', 'E0', 'R60', 'E1', 'R61', 'R50', 'E2',
+    'R51', 'R40', 'R41', 'W10', 'E3', 'W8', 'R30', 'R31', 'R20', 'R21', 'E4', 'E5', 'R10', 'R11', 'W4', 'R00', 'R01',
+    'W2', 'E6', 'T60', 'T61', 'T50', 'T51', 'T40', 'T41', 'T30', 'T31', 'T20', 'T21', 'T10', 'T11', 'F', 'T00', 'T01',
+)
 F32 = jnp.float32
 BF16 = jnp.bfloat16
 
@@ -288,7 +291,7 @@
 
     GATHER, SUMS, WORK, OWN, ALL = 0, 1, 2, 3, 63
     steps, arrived = [], [1, 0]
-    for word in ORDER.split():
+    for word in ORDER:
         kind, digits = word[0], word[1:]
         head = 1 if kind in 'ET' else 0
         if arrived[0] < n_hop:

time: 162 us -> 162 us (level)
  no operation moved by 1% of the time
where the time goes in v18:
time: 162 us
  Pallas kernels  161 us (99%)
    pallas_call x1, Pallas kernels, local_backward(): pl.pallas_call(functools.partial(ring_kernel, cp_size, sub_start, scale),...  159 us

profile of v18, /device:TPU:22, one launch (start us, length us, event | category | flops | bytes accessed | tf_op | source)
XLA Modules:
  0.0 161.9 jit_solution(15187036585945515706)
XLA Ops:
  0.6 158.7 %ring_backward.1 = (bf16[16,32,2,4,128]{4,3,2,1,0:T(4,128)(2,1)}, f32[640,2,128]{2,1,0:T(2,128)}, f32[640,2,128]{2,1,0:T(2,128)}) custom-call(bf16[640,2,128]{2,1,0:T(2,128)(2,1)} %k_in.1, bf16[640,2,128]{2,1,0:T(2,128)(2,1)} %v_in.1, bf16[16,32,2,4,128]{4,3,2,1,0:T(4,128)(2,1)} %bitcast.6, bf16[16,32,2,4,128]{4,3,2,1,0:T(4,128)(2,1)} %bitcast.7, ...), custom_call_target="tpu_custom_call" | custom-call | flops 46976204800 | bytes 31457280 | tf_op jit(solution)/shard_map/ring_backward/pallas_call | solution.py:438
  159.4 2.5 %results.1 = (bf16[16,32,2,4,128]{4,3,2,1,0:T(4,128)(2,1)}, f32[640,2,128]{2,1,0:T(2,128)}, f32[640,2,128]{2,1,0:T(2,128)}) custom-call(bf16[16,32,2,4,128]{4,3,2,1,0:T(4,128)(2,1)} %get-tuple-element.9.a, f32[640,2,128]{2,1,0:T(2,128)} %get-tuple-element.10.b, f32[640,2,128]{2,1,0:T(2,128)} %get-tuple-element.11.c), custom_call_target="tpu_custom_call" | custom-call | bytes 4194304 | tf_op jit(solution)/shard_map/results/pallas_call | solution.py:472
